TPU v7x, 32 devices: a whole 2x2x4 slice. The times are simulated.
32 devices in a mesh: region: 2 (over x), dev: 16 (over z, y, core).
Axes of the slice: x: 2, y: 2, z: 4, core: 2. Of those that a mesh axis runs over, the one named last changes fastest.
Arguments:
- object_field: float32 [2, 8192, 512], P(None, ('region', 'dev')), may hold values from -6 to 6
- probe: float32 [2, 256, 256], replicated, may hold values from -6 to 6
- amplitudes: float32 [2, 16, 4, 256, 256], P('region', 'dev'), may hold values from 0.5 to 4
- row_offset: int32 [2, 16, 4], P('region', 'dev'), may hold values from 0 to 255
- col_offset: int32 [2, 16, 4], P('region', 'dev'), may hold values from 0 to 256
- frame_count: int32 [2, 16], P('region', 'dev'), may hold values from 1 to 4, as said below
Outputs:
- new_object: float32 [2, 8192, 512], P(None, ('region', 'dev'))
- new_probe: float32 [2, 256, 256], replicated
Inputs may be any that keep to these rules, and one draw needn't show every extreme that they name: `frame_count`: in each region, device j and device j + 8 together hold at most 6 frames, and some device holds 4.
All inputs are finite; a program needn't handle non-finite values.
Results may differ from a plain program's by a relative error of at most 0.0003.
Values sent between devices are 32-bit elements; how exact they have to be, the bound alone decides.
A program may use at most 64 MiB of HBM per device.

v0:
```python
import math

import jax
import jax.numpy as jnp
import numpy as np
from jax import lax
from jax.experimental import pallas as pl
from jax.experimental.pallas import tpu as pltpu
from jax.sharding import PartitionSpec as P

PAD = 8


def from_behind(array, axis, by):
    peers = lax.axis_size(axis)
    pairs = [(i, i + by) for i in range(peers) if 0 <= i + by < peers]
    return lax.ppermute(array, axis, pairs)


def summed_over(array, axes):
    if any(lax.axis_size(axis) & (lax.axis_size(axis) - 1) for axis in axes):
        return lax.psum(array, axes)
    steps = []
    for axis in axes:
        size, bit = lax.axis_size(axis), 1
        while bit < size:
            steps.append((axis, bit, [(i, i ^ bit) for i in range(size)]))
            bit *= 2
    shape = array.shape
    share = array.reshape(-1, shape[-1])
    if share.shape[0] % (1 << len(steps)):
        return lax.psum(array, axes)
    for axis, bit, pairs in steps:
        half = share.shape[0] // 2
        upper = (lax.axis_index(axis) & bit) != 0
        low, high = share[:half], share[half:]
        arrived = lax.ppermute(jnp.where(upper, low, high), axis, pairs)
        share = jnp.where(upper, high, low) + arrived
    for axis, bit, pairs in reversed(steps):
        upper = (lax.axis_index(axis) & bit) != 0
        arrived = lax.ppermute(share, axis, pairs)
        share = jnp.concatenate([jnp.where(upper, arrived, share), jnp.where(upper, share, arrived)])
    return share.reshape(shape)


def split(x):
    high = x.astype(jnp.bfloat16)
    return high, (x - high.astype(jnp.float32)).astype(jnp.bfloat16)


def fourier_tables(length):
    index = np.arange(length)
    angle = (index[:, None] * index[None, :] % length) * (2.0 * math.pi / length)
    factor = 1.0 / math.sqrt(length)
    cosine = np.cos(angle) * factor
    sine = np.sin(angle) * factor
    parts = []
    for table in (cosine, sine, cosine + sine, cosine - sine):
        table = table.astype(np.float32)
        high = table.astype(jnp.bfloat16)
        parts += [high, (table - high.astype(np.float32)).astype(jnp.bfloat16)]
    return jnp.asarray(np.stack(parts))


def dot(a, b):
    return jnp.dot(a, b, preferred_element_type=jnp.float32)


def product(tables, which, x, left):
    t_high, t_low = tables[2 * which], tables[2 * which + 1]
    high, low = split(x)
    if left:
        return dot(t_high, high) + (dot(t_high, low) + dot(t_low, high))
    return dot(high, t_high) + (dot(low, t_high) + dot(high, t_low))


def side(tables, real, imag, inverse, left):
    first = product(tables, 2 if inverse else 3, real, left)
    second = product(tables, 0, imag - real, left)
    third = product(tables, 1, real + imag, left)
    if inverse:
        return first - third, first + second
    return first + third, first + second


def kernel(
    rows_s, cols_s, count_s, prior_s, field, rim, probe, measured, tables,
    totals, weight, grad, extended, spread,
):
    band, width = field.shape[1], field.shape[2]
    frame = probe.shape[1]
    slots = rows_s.shape[0]
    tall = frame + PAD
    extended[:, :band] = field[...]
    extended[:, band:] = rim[...]
    totals[...] = jnp.zeros_like(totals)
    spread[...] = jnp.zeros_like(spread)
    grad[...] = jnp.zeros_like(grad)

    def anchor(row):
        base = pl.multiple_of(row // PAD * PAD, PAD)
        return pl.ds(base, tall), row - base

    def cut(plane, row, col):
        at, shift = anchor(row)
        x = extended[plane, at, :]
        x = pltpu.roll(x, lax.rem(width - col, width), 1)[:, :frame]
        return pltpu.roll(x, lax.rem(tall - shift, tall), 0)[:frame]

    def place(x, row, col):
        at, shift = anchor(row)
        x = jnp.concatenate([x, jnp.zeros((PAD, frame), jnp.float32)], axis=0)
        x = pltpu.roll(x, shift, 0)
        x = jnp.concatenate([x, jnp.zeros((tall, width - frame), jnp.float32)], axis=1)
        return at, pltpu.roll(x, col, 1)

    def power():
        return probe[0] * probe[0] + probe[1] * probe[1]

    def prior(k, carry):
        at, x = place(power(), prior_s[k], prior_s[slots + k])
        spread[at, :] += x
        return carry

    lax.fori_loop(0, prior_s[2 * slots], prior, 0)
    weight[...] = spread[band:, :]
    spread[...] = jnp.zeros_like(spread)

    def one(k, carry):
        row, col = rows_s[k], cols_s[k]
        win_r, win_i = cut(0, row, col), cut(1, row, col)
        real = probe[0] * win_r - probe[1] * win_i
        imag = probe[0] * win_i + probe[1] * win_r
        real, imag = side(tables, real, imag, False, True)
        real, imag = side(tables, real, imag, False, False)
        factor = 1.0 - measured[k] * lax.rsqrt(real * real + imag * imag + 0.25)
        real, imag = side(tables, real * factor, imag * factor, True, True)
        real, imag = side(tables, real, imag, True, False)
        win_r, win_i = cut(0, row, col), cut(1, row, col)
        grad[0] += win_r * real + win_i * imag
        grad[1] += win_r * imag - win_i * real
        at, x = place(probe[0] * real + probe[1] * imag, row, col)
        totals[0, at, :] += x
        at, x = place(probe[0] * imag - probe[1] * real, row, col)
        totals[1, at, :] += x
        at, x = place(power(), row, col)
        spread[at, :] += x
        return carry

    lax.fori_loop(0, count_s[0], one, 0)
    weight[...] += spread[:band, :]


def on_device(object_field, probe, amplitudes, row_offset, col_offset, frame_count):
    _, band, width = object_field.shape
    frame = probe.shape[1]
    rows, cols, count = row_offset[0, 0], col_offset[0, 0], frame_count[0]
    rim = from_behind(object_field, "dev", -1)
    prior = from_behind(jnp.concatenate([rows, cols, count]), "dev", 1)
    smem = pl.BlockSpec(memory_space=pltpu.SMEM)
    vmem = pl.BlockSpec(memory_space=pltpu.VMEM)
    totals, weight, gradient = pl.pallas_call(
        kernel,
        out_shape=(
            jax.ShapeDtypeStruct((2, band + frame, width), jnp.float32),
            jax.ShapeDtypeStruct((band, width), jnp.float32),
            jax.ShapeDtypeStruct((2, frame, frame), jnp.float32),
        ),
        in_specs=[smem] * 4 + [vmem] * 5,
        out_specs=(vmem,) * 3,
        scratch_shapes=[
            pltpu.VMEM((2, band + frame, width), jnp.float32),
            pltpu.VMEM((band + frame, width), jnp.float32),
        ],
        compiler_params=pltpu.CompilerParams(vmem_limit_bytes=48 * 1024 * 1024),
    )(rows, cols, count, prior, object_field, rim, probe, amplitudes[0, 0], fourier_tables(frame))
    incoming = from_behind(totals[:, band:], "dev", 1)
    new_field = object_field - (totals[:, :band] + incoming) / (weight + 1.0)
    summed = summed_over(gradient, ("dev", "region"))
    step_scale = 0.25 / jnp.sqrt(jnp.sum(summed * summed) / summed.size + 1e-06)
    return new_field, probe - step_scale * summed


def solution(mesh):
    return jax.shard_map(
        on_device,
        mesh=mesh,
        in_specs=(
            P(None, ("region", "dev"), None),
            P(),
            P("region", "dev", None, None, None),
            P("region", "dev", None),
            P("region", "dev", None),
            P("region", "dev"),
        ),
        out_specs=(P(None, ("region", "dev"), None), P()),
        check_vma=False,
    )
```

profile of v0, /device:TPU:16, one launch (start us, length us, event | category | flops | bytes accessed | tf_op | source)
XLA Modules:
  0.0 97.4 jit_solution(18063475619313096454)
XLA Ops:
  0.6 2.8 %collective-permute-start.1 = (f32[2,256,512]{2,1,0:T(8,128)}, f32[2,256,512]{2,1,0:T(8,128)S(1)}, u32[]{:S(2)}, u32[]{:S(2)}) collective-permute-start(f32[2,256,512]{2,1,0:T(8,128)} %field.1), channel_id=1, source_target_pairs={{1,0},{2,1},{3,2},{4,3},{5,4},{6,5},{7,6},{8,7},{9,8},{10,9},{11,1... | collective-permute-start | bytes 3145736 | tf_op jit(solution)/shard_map/ppermute | solution.py:17
  4.0 0.7 pad_add_fusion
  4.8 1.9 %collective-permute-start = (s32[9]{0:T(128)S(1)}, s32[9]{0:T(128)S(1)}, u32[]{:S(2)}, u32[]{:S(2)}) collective-permute-start(s32[9]{0:T(128)S(1)} %pad_add_fusion), channel_id=1, source_target_pairs={{0,1},{1,2},{2,3},{3,4},{4,5},{5,6},{6,7},{7,8},{8,9},{9,10},{10,1... | collective-permute-start | bytes 116 | tf_op jit(solution)/shard_map/ppermute | solution.py:17
  6.7 3.9 %collective-permute-done.prior_s = s32[9]{0:T(128)S(1)} collective-permute-done((s32[9]{0:T(128)S(1)}, s32[9]{0:T(128)S(1)}, u32[]{:S(2)}, u32[]{:S(2)}) %collective-permute-start) | collective-permute-done | bytes 68 | tf_op jit(solution)/shard_map/ppermute | solution.py:17
  10.6 5.4 %collective-permute-done.1.rim = f32[2,256,512]{2,1,0:T(8,128)S(1)} collective-permute-done((f32[2,256,512]{2,1,0:T(8,128)}, f32[2,256,512]{2,1,0:T(8,128)S(1)}, u32[]{:S(2)}, u32[]{:S(2)}) %collective-permute-start.1) | collective-permute-done | bytes 1048608 | tf_op jit(solution)/shard_map/ppermute | solution.py:17
  16.0 0.0 copy-start
  16.0 1.2 %copy-done = f32[2,256,512]{2,1,0:T(8,128)S(1)} copy-done((f32[2,256,512]{2,1,0:T(8,128)S(1)}, f32[2,256,512]{2,1,0:T(8,128)}, u32[]{:S(2)}) %copy-start) | copy-done | bytes 1048600
  17.2 0.0 copy-start.2
  17.2 1.0 %copy-done.2 = f32[2,256,256]{2,1,0:T(8,128)S(1)} copy-done((f32[2,256,256]{2,1,0:T(8,128)S(1)}, f32[2,256,256]{2,1,0:T(8,128)}, u32[]{:S(2)}) %copy-start.2) | copy-done | bytes 524312
  18.3 0.0 copy-start.4
  18.3 1.2 %copy-done.4 = f32[1,1,4,256,256]{4,3,2,1,0:T(8,128)S(1)} copy-done((f32[1,1,4,256,256]{4,3,2,1,0:T(8,128)S(1)}, f32[1,1,4,256,256]{4,3,2,1,0:T(8,128)}, u32[]{:S(2)}) %copy-start.4) | copy-done | bytes 1048600
  19.5 1.2 %copy-done.5 = bf16[8,256,256]{2,1,0:T(8,128)(2,1)S(1)} copy-done((bf16[8,256,256]{2,1,0:T(8,128)(2,1)S(1)}, bf16[8,256,256]{2,1,0:T(8,128)(2,1)}, u32[]{:S(2)}) %copy-start.5) | copy-done | bytes 1048600
  20.7 0.7 copy-done.6
  21.4 0.7 copy-done.7
  22.0 9.7 %shard_map.86 = (f32[2,512,512]{2,1,0:T(8,128)}, f32[256,512]{1,0:T(8,128)S(1)}, f32[2,256,256]{2,1,0:T(8,128)S(1)}) custom-call(s32[4]{0:T(128)S(1)} %bitcast.13, s32[4]{0:T(128)S(1)} %bitcast.15, s32[1]{0:T(128)} %bitcast.10.count_s, s32[9]{0:T(128)S(1)} %collective-permute-done.prior_s, f32[2,256,512]{2,1,0:T(8,128)S(1)} %copy-done, ...), custom_call_target="tpu_custom_call" | custom-call | tf_op jit(solution)/shard_map/pallas_call | solution.py:162
  31.8 0.6 collective-permute-start.3
  32.4 1.2 %collective-permute-done.3 = f32[256,256]{1,0:T(8,128)S(1)} collective-permute-done((f32[256,256]{1,0:T(8,128)S(1)}, f32[256,256]{1,0:T(8,128)S(1)}, u32[]{:S(2)}, u32[]{:S(2)}) %collective-permute-start.3) | collective-permute-done | bytes 262176 | tf_op jit(solution)/shard_map/ppermute | solution.py:37
  33.6 0.1 bitcast_add_fusion
  33.7 9.2 %collective-permute-start.4 = (f32[128,256]{1,0:T(8,128)S(1)}, f32[128,256]{1,0:T(8,128)S(1)}, u32[]{:S(2)}, u32[]{:S(2)}) collective-permute-start(f32[128,256]{1,0:T(8,128)S(1)} %slice_select_fusion), channel_id=1, source_target_pairs={{0,2},{1,3},{2,0},{3,1},{4,6},{5,7},{6,4},{7,5},{8,10},{9,11},{10,... | collective-permute-start | bytes 393224 | tf_op jit(solution)/shard_map/ppermute | solution.py:37
  42.9 4.0 %collective-permute-done.4 = f32[128,256]{1,0:T(8,128)S(1)} collective-permute-done((f32[128,256]{1,0:T(8,128)S(1)}, f32[128,256]{1,0:T(8,128)S(1)}, u32[]{:S(2)}, u32[]{:S(2)}) %collective-permute-start.4) | collective-permute-done | bytes 131104 | tf_op jit(solution)/shard_map/ppermute | solution.py:37
  46.9 0.1 collective-permute-start.5
  47.0 4.2 %collective-permute-done.5 = f32[64,256]{1,0:T(8,128)S(1)} collective-permute-done((f32[64,256]{1,0:T(8,128)S(1)}, f32[64,256]{1,0:T(8,128)S(1)}, u32[]{:S(2)}, u32[]{:S(2)}) %collective-permute-start.5) | collective-permute-done | bytes 65568 | tf_op jit(solution)/shard_map/ppermute | solution.py:37
  51.3 0.1 collective-permute-start.6
  51.4 4.8 %collective-permute-done.6 = f32[32,256]{1,0:T(8,128)S(1)} collective-permute-done((f32[32,256]{1,0:T(8,128)S(1)}, f32[32,256]{1,0:T(8,128)S(1)}, u32[]{:S(2)}, u32[]{:S(2)}) %collective-permute-start.6) | collective-permute-done | bytes 32800 | tf_op jit(solution)/shard_map/ppermute | solution.py:37
  56.2 1.3 %collective-permute-start.7 = (f32[16,256]{1,0:T(8,128)S(1)}, f32[16,256]{1,0:T(8,128)S(1)}, u32[]{:S(2)}, u32[]{:S(2)}) collective-permute-start(f32[16,256]{1,0:T(8,128)S(1)} %slice_select_fusion.3), channel_id=1, source_target_pairs={{0,16},{16,0},{1,17},{17,1},{2,18},{18,2},{3,19},{19,3},{4,20},{20... | collective-permute-start | bytes 49160 | tf_op jit(solution)/shard_map/ppermute | solution.py:37
  57.5 2.5 %collective-permute-done.7 = f32[16,256]{1,0:T(8,128)S(1)} collective-permute-done((f32[16,256]{1,0:T(8,128)S(1)}, f32[16,256]{1,0:T(8,128)S(1)}, u32[]{:S(2)}, u32[]{:S(2)}) %collective-permute-start.7) | collective-permute-done | bytes 16416 | tf_op jit(solution)/shard_map/ppermute | solution.py:37
  60.0 1.2 %collective-permute-start.8 = (f32[16,256]{1,0:T(8,128)S(1)}, f32[16,256]{1,0:T(8,128)S(1)}, u32[]{:S(2)}, u32[]{:S(2)}) collective-permute-start(f32[16,256]{1,0:T(8,128)S(1)} %select_add_fusion.3), channel_id=1, source_target_pairs={{0,16},{16,0},{1,17},{17,1},{2,18},{18,2},{3,19},{19,3},{4,20},{20... | collective-permute-start | bytes 49160 | tf_op jit(solution)/shard_map/ppermute | solution.py:41
  61.2 2.5 %collective-permute-done.8 = f32[16,256]{1,0:T(8,128)S(1)} collective-permute-done((f32[16,256]{1,0:T(8,128)S(1)}, f32[16,256]{1,0:T(8,128)S(1)}, u32[]{:S(2)}, u32[]{:S(2)}) %collective-permute-start.8) | collective-permute-done | bytes 16416 | tf_op jit(solution)/shard_map/ppermute | solution.py:41
  63.8 0.1 collective-permute-start.9
  63.8 4.8 %collective-permute-done.9 = f32[32,256]{1,0:T(8,128)S(1)} collective-permute-done((f32[32,256]{1,0:T(8,128)S(1)}, f32[32,256]{1,0:T(8,128)S(1)}, u32[]{:S(2)}, u32[]{:S(2)}) %collective-permute-start.9) | collective-permute-done | bytes 32800 | tf_op jit(solution)/shard_map/ppermute | solution.py:41
  68.7 0.1 collective-permute-start.10
  68.7 4.3 %collective-permute-done.10 = f32[64,256]{1,0:T(8,128)S(1)} collective-permute-done((f32[64,256]{1,0:T(8,128)S(1)}, f32[64,256]{1,0:T(8,128)S(1)}, u32[]{:S(2)}, u32[]{:S(2)}) %collective-permute-start.10) | collective-permute-done | bytes 65568 | tf_op jit(solution)/shard_map/ppermute | solution.py:41
  73.0 2.2 %collective-permute-start.11 = (f32[128,256]{1,0:T(8,128)S(1)}, f32[128,256]{1,0:T(8,128)S(1)}, u32[]{:S(2)}, u32[]{:S(2)}) collective-permute-start(f32[128,256]{1,0:T(8,128)S(1)} %pad_maximum_fusion.2), channel_id=1, source_target_pairs={{0,2},{1,3},{2,0},{3,1},{4,6},{5,7},{6,4},{7,5},{8,10},{9,11},{10,... | collective-permute-start | bytes 393224 | tf_op jit(solution)/shard_map/ppermute | solution.py:41
  75.2 2.3 %slice.39 = f32[2,256,512]{2,1,0:T(8,128)} slice(f32[2,512,512]{2,1,0:T(8,128)} %get-tuple-element.5), slice={[0:2], [256:512], [0:512]} | slice | bytes 2097152 | tf_op jit(solution)/shard_map/slice | solution.py:177
  77.5 1.9 %collective-permute-start.2 = (f32[2,256,512]{2,1,0:T(8,128)}, f32[2,256,512]{2,1,0:T(8,128)}, u32[]{:S(2)}, u32[]{:S(2)}) collective-permute-start(f32[2,256,512]{2,1,0:T(8,128)} %slice.39), channel_id=1, source_target_pairs={{0,1},{1,2},{2,3},{3,4},{4,5},{5,6},{6,7},{7,8},{8,9},{9,10},{10,1... | collective-permute-start | bytes 3145736 | tf_op jit(solution)/shard_map/ppermute | solution.py:17
  79.4 0.0 collective-permute-done.11
  79.4 0.0 copy-start.3
  79.5 0.2 collective-permute-start.12
  79.7 0.0 copy-start.1
  79.7 2.5 %collective-permute-done.12 = f32[256,256]{1,0:T(8,128)S(1)} collective-permute-done((f32[256,256]{1,0:T(8,128)S(1)}, f32[256,256]{1,0:T(8,128)S(1)}, u32[]{:S(2)}, u32[]{:S(2)}) %collective-permute-start.12) | collective-permute-done | bytes 262176 | tf_op jit(solution)/shard_map/ppermute | solution.py:41
  82.3 0.7 multiply_reduce_fusion
  83.7 0.0 copy-start.8
  83.7 0.0 copy-done.3
  83.8 0.9 sub.7
  84.6 10.2 %collective-permute-done.2 = f32[2,256,512]{2,1,0:T(8,128)} collective-permute-done((f32[2,256,512]{2,1,0:T(8,128)}, f32[2,256,512]{2,1,0:T(8,128)}, u32[]{:S(2)}, u32[]{:S(2)}) %collective-permute-start.2) | collective-permute-done | bytes 1048608 | tf_op jit(solution)/shard_map/ppermute | solution.py:17
  94.8 0.0 copy-done.1
  94.8 0.0 copy-done.8
  94.8 2.6 %divide_subtract_fusion = f32[2,256,512]{2,1,0:T(8,128)} fusion(f32[2,256,512]{2,1,0:T(8,128)S(1)} %copy-done.1, f32[2,256,512]{2,1,0:T(8,128)} %collective-permute-done.2, f32[2,512,512]{2,1,0:T(8,128)S(1)} %copy-done.8, f32[256,512]{1,0:T(8,128)S(1)} %broadcast_add_fusion), kind=kLoop, calls=%fused_computation | loop fusion | flops 786432 | bytes 4718592 | tf_op jit(solution)/shard_map/sub | solution.py:178
  (23 shorter events, 0.3 us)
Async XLA Ops:
  0.6 15.4 %collective-permute-start.1 = (f32[2,256,512]{2,1,0:T(8,128)}, f32[2,256,512]{2,1,0:T(8,128)S(1)}, u32[]{:S(2)}, u32[]{:S(2)}) collective-permute-start(f32[2,256,512]{2,1,0:T(8,128)} %field.1), channel_id=1, source_target_pairs={{1,0},{2,1},{3,2},{4,3},{5,4},{6,5},{7,6},{8,7},{9,8},{10,9},{11,1... | collective-permute-start | bytes 3145736 | tf_op jit(solution)/shard_map/ppermute | solution.py:17
  4.8 5.8 %collective-permute-start = (s32[9]{0:T(128)S(1)}, s32[9]{0:T(128)S(1)}, u32[]{:S(2)}, u32[]{:S(2)}) collective-permute-start(s32[9]{0:T(128)S(1)} %pad_add_fusion), channel_id=1, source_target_pairs={{0,1},{1,2},{2,3},{3,4},{4,5},{5,6},{6,7},{7,8},{8,9},{9,10},{10,1... | collective-permute-start | bytes 116 | tf_op jit(solution)/shard_map/ppermute | solution.py:17
  16.0 1.2 %copy-start = (f32[2,256,512]{2,1,0:T(8,128)S(1)}, f32[2,256,512]{2,1,0:T(8,128)}, u32[]{:S(2)}) copy-start(f32[2,256,512]{2,1,0:T(8,128)} %field.1) | copy-start | bytes 3145732
  17.2 1.0 %copy-start.2 = (f32[2,256,256]{2,1,0:T(8,128)S(1)}, f32[2,256,256]{2,1,0:T(8,128)}, u32[]{:S(2)}) copy-start(f32[2,256,256]{2,1,0:T(8,128)} %probe.1) | copy-start | bytes 1572868
  18.3 1.2 %copy-start.4 = (f32[1,1,4,256,256]{4,3,2,1,0:T(8,128)S(1)}, f32[1,1,4,256,256]{4,3,2,1,0:T(8,128)}, u32[]{:S(2)}) copy-start(f32[1,1,4,256,256]{4,3,2,1,0:T(8,128)} %param.9) | copy-start | bytes 3145732
  19.5 1.2 %copy-start.5 = (bf16[8,256,256]{2,1,0:T(8,128)(2,1)S(1)}, bf16[8,256,256]{2,1,0:T(8,128)(2,1)}, u32[]{:S(2)}) copy-start(bf16[8,256,256]{2,1,0:T(8,128)(2,1)} %constant.32.clone.tables) | copy-start | bytes 3145732
  20.7 0.7 copy-start.6
  21.4 0.7 copy-start.7
  31.8 1.8 %collective-permute-start.3 = (f32[256,256]{1,0:T(8,128)S(1)}, f32[256,256]{1,0:T(8,128)S(1)}, u32[]{:S(2)}, u32[]{:S(2)}) collective-permute-start(f32[256,256]{1,0:T(8,128)S(1)} %select_bitcast_fusion), channel_id=1, source_target_pairs={{0,1},{1,0},{2,3},{3,2},{4,5},{5,4},{6,7},{7,6},{8,9},{9,8},{10,11... | collective-permute-start | bytes 786440 | tf_op jit(solution)/shard_map/ppermute | solution.py:37
  33.7 13.2 %collective-permute-start.4 = (f32[128,256]{1,0:T(8,128)S(1)}, f32[128,256]{1,0:T(8,128)S(1)}, u32[]{:S(2)}, u32[]{:S(2)}) collective-permute-start(f32[128,256]{1,0:T(8,128)S(1)} %slice_select_fusion), channel_id=1, source_target_pairs={{0,2},{1,3},{2,0},{3,1},{4,6},{5,7},{6,4},{7,5},{8,10},{9,11},{10,... | collective-permute-start | bytes 393224 | tf_op jit(solution)/shard_map/ppermute | solution.py:37
  46.9 4.3 %collective-permute-start.5 = (f32[64,256]{1,0:T(8,128)S(1)}, f32[64,256]{1,0:T(8,128)S(1)}, u32[]{:S(2)}, u32[]{:S(2)}) collective-permute-start(f32[64,256]{1,0:T(8,128)S(1)} %slice_select_fusion.1), channel_id=1, source_target_pairs={{0,4},{1,5},{2,6},{3,7},{4,0},{5,1},{6,2},{7,3},{8,12},{9,13},{10,... | collective-permute-start | bytes 196616 | tf_op jit(solution)/shard_map/ppermute | solution.py:37
  51.3 4.9 %collective-permute-start.6 = (f32[32,256]{1,0:T(8,128)S(1)}, f32[32,256]{1,0:T(8,128)S(1)}, u32[]{:S(2)}, u32[]{:S(2)}) collective-permute-start(f32[32,256]{1,0:T(8,128)S(1)} %slice_select_fusion.2), channel_id=1, source_target_pairs={{0,8},{1,9},{2,10},{3,11},{4,12},{5,13},{6,14},{7,15},{8,0},{9,1},... | collective-permute-start | bytes 98312 | tf_op jit(solution)/shard_map/ppermute | solution.py:37
  56.2 3.8 %collective-permute-start.7 = (f32[16,256]{1,0:T(8,128)S(1)}, f32[16,256]{1,0:T(8,128)S(1)}, u32[]{:S(2)}, u32[]{:S(2)}) collective-permute-start(f32[16,256]{1,0:T(8,128)S(1)} %slice_select_fusion.3), channel_id=1, source_target_pairs={{0,16},{16,0},{1,17},{17,1},{2,18},{18,2},{3,19},{19,3},{4,20},{20... | collective-permute-start | bytes 49160 | tf_op jit(solution)/shard_map/ppermute | solution.py:37
  60.0 3.7 %collective-permute-start.8 = (f32[16,256]{1,0:T(8,128)S(1)}, f32[16,256]{1,0:T(8,128)S(1)}, u32[]{:S(2)}, u32[]{:S(2)}) collective-permute-start(f32[16,256]{1,0:T(8,128)S(1)} %select_add_fusion.3), channel_id=1, source_target_pairs={{0,16},{16,0},{1,17},{17,1},{2,18},{18,2},{3,19},{19,3},{4,20},{20... | collective-permute-start | bytes 49160 | tf_op jit(solution)/shard_map/ppermute | solution.py:41
  63.8 4.9 %collective-permute-start.9 = (f32[32,256]{1,0:T(8,128)S(1)}, f32[32,256]{1,0:T(8,128)S(1)}, u32[]{:S(2)}, u32[]{:S(2)}) collective-permute-start(f32[32,256]{1,0:T(8,128)S(1)} %pad_maximum_fusion.4), channel_id=1, source_target_pairs={{0,8},{1,9},{2,10},{3,11},{4,12},{5,13},{6,14},{7,15},{8,0},{9,1},... | collective-permute-start | bytes 98312 | tf_op jit(solution)/shard_map/ppermute | solution.py:41
  68.7 4.3 %collective-permute-start.10 = (f32[64,256]{1,0:T(8,128)S(1)}, f32[64,256]{1,0:T(8,128)S(1)}, u32[]{:S(2)}, u32[]{:S(2)}) collective-permute-start(f32[64,256]{1,0:T(8,128)S(1)} %pad_maximum_fusion.3), channel_id=1, source_target_pairs={{0,4},{1,5},{2,6},{3,7},{4,0},{5,1},{6,2},{7,3},{8,12},{9,13},{10,... | collective-permute-start | bytes 196616 | tf_op jit(solution)/shard_map/ppermute | solution.py:41
  73.0 6.3 %collective-permute-start.11 = (f32[128,256]{1,0:T(8,128)S(1)}, f32[128,256]{1,0:T(8,128)S(1)}, u32[]{:S(2)}, u32[]{:S(2)}) collective-permute-start(f32[128,256]{1,0:T(8,128)S(1)} %pad_maximum_fusion.2), channel_id=1, source_target_pairs={{0,2},{1,3},{2,0},{3,1},{4,6},{5,7},{6,4},{7,5},{8,10},{9,11},{10,... | collective-permute-start | bytes 393224 | tf_op jit(solution)/shard_map/ppermute | solution.py:41
  77.5 17.3 %collective-permute-start.2 = (f32[2,256,512]{2,1,0:T(8,128)}, f32[2,256,512]{2,1,0:T(8,128)}, u32[]{:S(2)}, u32[]{:S(2)}) collective-permute-start(f32[2,256,512]{2,1,0:T(8,128)} %slice.39), channel_id=1, source_target_pairs={{0,1},{1,2},{2,3},{3,4},{4,5},{5,6},{6,7},{7,8},{8,9},{9,10},{10,1... | collective-permute-start | bytes 3145736 | tf_op jit(solution)/shard_map/ppermute | solution.py:17
  79.4 4.3 %copy-start.3 = (f32[2,256,256]{2,1,0:T(8,128)S(1)}, f32[2,256,256]{2,1,0:T(8,128)}, u32[]{:S(2)}) copy-start(f32[2,256,256]{2,1,0:T(8,128)} %probe.1) | copy-start | bytes 1572868
  79.5 2.8 %collective-permute-start.12 = (f32[256,256]{1,0:T(8,128)S(1)}, f32[256,256]{1,0:T(8,128)S(1)}, u32[]{:S(2)}, u32[]{:S(2)}) collective-permute-start(f32[256,256]{1,0:T(8,128)S(1)} %pad_maximum_fusion.1), channel_id=1, source_target_pairs={{0,1},{1,0},{2,3},{3,2},{4,5},{5,4},{6,7},{7,6},{8,9},{9,8},{10,11... | collective-permute-start | bytes 786440 | tf_op jit(solution)/shard_map/ppermute | solution.py:41
  79.7 15.1 %copy-start.1 = (f32[2,256,512]{2,1,0:T(8,128)S(1)}, f32[2,256,512]{2,1,0:T(8,128)}, u32[]{:S(2)}) copy-start(f32[2,256,512]{2,1,0:T(8,128)} %field.1) | copy-start | bytes 3145732
  83.7 11.1 %copy-start.8 = (f32[2,512,512]{2,1,0:T(8,128)S(1)}, f32[2,512,512]{2,1,0:T(8,128)}, u32[]{:S(2)}) copy-start(f32[2,512,512]{2,1,0:T(8,128)} %get-tuple-element.5) | copy-start | bytes 6291460
where the time goes:
time: 97.7 us; the launch traced here: 97.4 us
  waiting for transfers between devices  50.3 us (51%)
  starting transfers between devices  21.5 us (22%)
  Pallas kernels  9.74 us (10%)
  local copies, waits for them, and re-layouts  8.3 us (8%)
  other arithmetic  5.34 us (5%)
  between operations  2.19 us (2%)
    ppermute x3, waiting for transfers between devices, from_behind(): return lax.ppermute(array, axis, pairs)  19.4 us
    ppermute x5, waiting for transfers between devices, summed_over(): arrived = lax.ppermute(jnp.where(upper, low, high), axis, pairs)  16.8 us
    ppermute x5, waiting for transfers between devices, summed_over(): arrived = lax.ppermute(share, axis, pairs)  14.1 us
    ppermute x5, starting transfers between devices, summed_over(): arrived = lax.ppermute(jnp.where(upper, low, high), axis, pairs)  11.2 us
    pallas_call x1, Pallas kernels, on_device(): pl.pallas_call(kernel, out_shape=(jax.ShapeDtypeStruct((2, band + frame,...  9.74 us
    ppermute x3, starting transfers between devices, from_behind(): return lax.ppermute(array, axis, pairs)  6.58 us
    unnamed x18, local copies, waits for them, and re-layouts  6.04 us
    ppermute x5, starting transfers between devices, summed_over(): arrived = lax.ppermute(share, axis, pairs)  3.69 us
  transfers between devices with their start and end apart: 13, of which 12 were waited for; matrix products, arithmetic and copies ran while one was open for 5% of the time, Pallas kernels for 0%

commit v1 on v0

v1 whole, which is shorter than its diff:
```python
import functools
import math

import jax
import jax.numpy as jnp
import numpy as np
from jax import lax
from jax.experimental import pallas as pl
from jax.experimental.pallas import tpu as pltpu
from jax.sharding import PartitionSpec as P

MESH = pl.DeviceIdType.MESH
SPREAD = 4
TILE = 8
CHUNKS = 4
STRIP = 16


def halves(x):
    high = x.astype(jnp.bfloat16)
    return high, (x - high.astype(jnp.float32)).astype(jnp.bfloat16)


def fourier_tables(length):
    half = length // 2
    m, q = np.arange(half)[:, None], np.arange(half)[None, :]
    tables = []
    for odd in (0, 1):
        angle = -(m * (2 * q + odd) % length) * (2.0 * math.pi / length)
        cosine, sine = np.cos(angle) / math.sqrt(length), np.sin(angle) / math.sqrt(length)
        tables.append(np.block([[cosine, sine], [-sine, cosine]]))
    parts = []
    for table in tables + [table.T for table in tables]:
        high = table.astype(jnp.bfloat16)
        parts.append(np.stack([high, (table - high.astype(np.float64)).astype(jnp.bfloat16)]))
    return jnp.asarray(np.stack(parts))


def times_right(x, tables, which):
    high, low = halves(x)
    t_high, t_low = tables[which, 0], tables[which, 1]
    return jnp.dot(
        jnp.concatenate([high, low, high], axis=1),
        jnp.concatenate([t_high, t_high, t_low], axis=0),
        preferred_element_type=jnp.float32,
    )


def times_left(tables, which, x):
    high, low = halves(x)
    t_high, t_low = tables[which, 0], tables[which, 1]
    return jnp.dot(
        jnp.concatenate([t_high, t_high, t_low], axis=1),
        jnp.concatenate([high, low, high], axis=0),
        preferred_element_type=jnp.float32,
    )


def bit_of(index, weight):
    return lax.rem(lax.div(index, weight), 2)


def flipped(index, weight):
    return index + weight * (1 - 2 * bit_of(index, weight))


def flipped_by(index, number):
    weight = 1
    while weight <= number:
        if number & weight:
            index = flipped(index, weight)
        weight *= 2
    return index


def remote(src, dst, send, recv, device):
    return pltpu.make_async_remote_copy(
        src_ref=src, dst_ref=dst, send_sem=send, recv_sem=recv, device_id=device, device_id_type=MESH
    )


class Plan:
    def __init__(self, regions, devs, frame):
        self.regions, self.devs = regions, devs
        self.stride = devs // SPREAD
        self.rows = frame // SPREAD
        pairs = [("region", 1 << b) for b in range(regions.bit_length() - 1)]
        pairs += [("dev", 1 << b) for b in range(1, self.stride.bit_length() - 1)]
        most = (self.rows // TILE).bit_length() - 1
        self.scatter, self.double = pairs[:most], pairs[most:]
        self.sizes = [self.rows >> i for i in range(len(self.scatter) + 1)]
        self.piece = self.sizes[-1]


def kernel(plan, rows_s, cols_s, count_s, field_h, probe_h, amps_h, tables_h, new_field, new_probe, *scratch):
    (
        prior_rows, prior_cols, prior_count, field, rim, probe, amps, tables, rolled, window, wanted, spec, back,
        left_side, weight, total, ahead, arrived, grad, halved, whole, final, gathered,
    ) = scratch[:23]
    rest = list(scratch[23:])
    came = [rest.pop(0) for _ in plan.scatter]
    held = [rest.pop(0) for _ in plan.scatter]
    twice = [rest.pop(0) for _ in plan.double]
    given = [rest.pop(0) for _ in plan.double]
    local, rim_sem, prior_sem, total_sem, core_sem, pair_sem, z_sem, double_sem, zback_sem, pback_sem, cback_sem = rest
    region, dev = lax.axis_index("region"), lax.axis_index("dev")
    devs = plan.devs
    slots, frame = amps.shape[0], probe.shape[1]
    half = frame // 2
    band = field.shape[1]
    core = lax.rem(dev, 2)
    z = lax.div(dev, plan.stride)

    def partner(pair):
        axis, weight_ = pair
        if axis == "region":
            return (flipped(region, weight_), dev)
        return (region, flipped(dev, weight_))

    def across(other):
        return (region, lax.rem(dev, plan.stride) + other * plan.stride)

    sibling = partner(("dev", 1))
    behind = (region, lax.rem(dev + devs - 1, devs))
    beyond = (region, lax.rem(dev + 1, devs))

    loads = []
    for i, (src, dst) in enumerate(((probe_h, probe), (field_h, field), (amps_h, amps), (tables_h, tables))):
        loads.append(pltpu.make_async_copy(src, dst, local.at[i]))
        loads[-1].start()

    peers = [sibling, behind, beyond] + [partner(p) for p in plan.scatter + plan.double]
    peers += [across(flipped_by(z, t)) for t in range(1, SPREAD)]
    barrier = pltpu.get_barrier_semaphore()
    for peer in peers:
        pl.semaphore_signal(barrier, inc=1, device_id=peer, device_id_type=MESH)
    pl.semaphore_wait(barrier, len(peers))

    step = band // CHUNKS

    def rim_copy(c):
        rows = pl.ds(c * step, step)
        return remote(field_h.at[:, rows, :], rim.at[:, rows, :], rim_sem.at[0, c], rim_sem.at[1, c], behind)

    def prior_copy(i):
        src = (rows_s, cols_s, count_s)[i]
        dst = (prior_rows, prior_cols, prior_count)[i]
        return remote(src, dst, prior_sem.at[0, i], prior_sem.at[1, i], beyond)

    def total_copy(c):
        rows = pl.ds(c * step, step)
        return remote(ahead.at[:, rows, :], arrived.at[:, rows, :], total_sem.at[0, c], total_sem.at[1, c], beyond)

    has_next, has_prior = dev < devs - 1, dev > 0

    @pl.when(has_prior)
    def _():
        for c in range(CHUNKS):
            rim_copy(c).start()

    @pl.when(has_next)
    def _():
        for i in range(3):
            prior_copy(i).start()

    @pl.when(dev == devs - 1)
    def _():
        rim[...] = jnp.zeros_like(rim)

    @pl.when(dev == 0)
    def _():
        arrived[...] = jnp.zeros_like(arrived)
        for i in range(slots):
            prior_rows[i] = 0
            prior_cols[i] = 0
        prior_count[0] = 0

    row_at = lax.broadcasted_iota(jnp.int32, (frame, frame), 0)
    col_at = lax.broadcasted_iota(jnp.int32, (frame, frame), 1)

    def live(k, count):
        return jnp.where(k < count, jnp.float32(1.0), jnp.float32(0.0))

    def turned(x, row, col):
        return pltpu.roll(pltpu.roll(x, row, 0), lax.rem(col, frame), 1)

    def turned_back(x, row, col):
        x = pltpu.roll(x, lax.rem(2 * frame - col, frame), 1)
        return pltpu.roll(x, lax.rem(frame - row, frame), 0)

    loads[0].wait()
    weight[...] = jnp.zeros_like(weight)

    def prepare(k, carry):
        row, col = rows_s[k], cols_s[k]
        real, imag = turned(probe[0], row, col), turned(probe[1], row, col)
        rolled[k, 0] = real
        rolled[k, 1] = imag
        power = (real * real + imag * imag) * live(k, count_s[0])
        power = jnp.where(row_at >= row, power, 0.0)
        weight[:, :frame] += jnp.where(col_at >= col, power, 0.0)
        weight[:, frame:] += jnp.where(col_at >= col, 0.0, power)
        return carry

    lax.fori_loop(0, slots, prepare, 0)
    loads[2].wait()

    def picked(source, place):
        order = 2 * place - jnp.where(place >= half, frame - 1, 0)
        return jnp.where(source == order, 1.0, 0.0).astype(jnp.bfloat16)

    picks, picks_t = picked(row_at, col_at), picked(col_at, row_at)

    def arrange(k, carry):
        high, low = halves(amps[k])
        x = jnp.dot(
            jnp.concatenate([picks_t, picks_t], axis=1),
            jnp.concatenate([high, low], axis=0),
            preferred_element_type=jnp.float32,
        )
        high, low = halves(x)
        wanted[k] = jnp.dot(
            jnp.concatenate([high, low], axis=1),
            jnp.concatenate([picks, picks], axis=0),
            preferred_element_type=jnp.float32,
        )
        return carry

    lax.fori_loop(0, slots, arrange, 0)

    @pl.when(has_prior)
    def _():
        for i in range(3):
            prior_copy(i).wait_recv()

    def prior(k, carry):
        row, col = prior_rows[k], prior_cols[k]
        power = probe[0] * probe[0] + probe[1] * probe[1]
        power = turned(power, row, col) * live(k, prior_count[0])
        power = jnp.where(row_at < row, power, 0.0)
        weight[:, :frame] += jnp.where(col_at >= col, power, 0.0)
        weight[:, frame:] += jnp.where(col_at >= col, 0.0, power)
        return carry

    lax.fori_loop(0, slots, prior, 0)
    loads[1].wait()
    loads[3].wait()

    def first(c, carry):
        @pl.when(has_next)
        def _():
            rim_copy(c).wait_recv()

        start = pl.multiple_of(c * step, step)
        rows = pl.ds(start, step)
        at = start + lax.broadcasted_iota(jnp.int32, (step, width), 0)
        for k in range(slots):
            row, col = rows_s[k], cols_s[k]
            pieces = []
            for plane in (0, 1):
                x = jnp.where(at >= row, field[plane, rows, :], rim[plane, rows, :])
                x = jnp.where(col_at[:step] >= col, x[:, :frame], x[:, frame:])
                window[k, plane, rows, :] = x
                pieces.append(x)
            p_r, p_i = rolled[k, 0, rows, :], rolled[k, 1, rows, :]
            real = p_r * pieces[0] - p_i * pieces[1]
            imag = p_r * pieces[1] + p_i * pieces[0]
            add = jnp.concatenate([real[:, :half] + real[:, half:], imag[:, :half] + imag[:, half:]], axis=1)
            sub = jnp.concatenate([real[:, :half] - real[:, half:], imag[:, :half] - imag[:, half:]], axis=1)
            for i, x in enumerate((add, sub)):
                high, low = halves(x)
                left_side[i, k * step:(k + 1) * step, :frame] = high
                left_side[i, k * step:(k + 1) * step, frame:2 * frame] = low
                left_side[i, k * step:(k + 1) * step, 2 * frame:] = high
        for i in (0, 1):
            out = jnp.dot(
                left_side[i],
                jnp.concatenate([tables[i, 0], tables[i, 0], tables[i, 1]], axis=0),
                preferred_element_type=jnp.float32,
            )
            for k in range(slots):
                for plane in (0, 1):
                    spec[k, plane, rows, i * half:(i + 1) * half] = out[
                        k * step:(k + 1) * step, plane * half:(plane + 1) * half
                    ]
        return carry

    width = field.shape[2]
    lax.fori_loop(0, CHUNKS, first, 0)
    grad[...] = jnp.zeros_like(grad)

    def one(k, carry):
        real, imag = spec[k, 0], spec[k, 1]
        add = jnp.concatenate([real[:half] + real[half:], imag[:half] + imag[half:]], axis=0)
        sub = jnp.concatenate([real[:half] - real[half:], imag[:half] - imag[half:]], axis=0)
        sides = []
        for i, x in enumerate((add, sub)):
            x = times_left(tables, 2 + i, x)
            real, imag = x[:half], x[half:]
            factor = 1.0 - wanted[k, i * half:(i + 1) * half, :] * lax.rsqrt(real * real + imag * imag + 0.25)
            x = jnp.concatenate([real * factor, imag * factor], axis=0)
            sides.append(times_left(tables, i, x))
        add, sub = sides[0] + sides[1], sides[0] - sides[1]
        real = jnp.concatenate([add[:half], sub[:half]], axis=0)
        imag = jnp.concatenate([add[half:], sub[half:]], axis=0)
        even = times_right(jnp.concatenate([real[:, :half], imag[:, :half]], axis=1), tables, 2)
        odd = times_right(jnp.concatenate([real[:, half:], imag[:, half:]], axis=1), tables, 3)
        alive = live(k, count_s[0])
        add, sub = (even + odd) * alive, (even - odd) * alive
        real = jnp.concatenate([add[:, :half], sub[:, :half]], axis=1)
        imag = jnp.concatenate([add[:, half:], sub[:, half:]], axis=1)
        back[k, 0] = real
        back[k, 1] = imag
        w_r, w_i = window[k, 0], window[k, 1]
        row, col = rows_s[k], cols_s[k]
        shape = grad.shape[1:]
        grad[0] += turned_back(w_r * real + w_i * imag, row, col).reshape(shape)
        grad[1] += turned_back(w_r * imag - w_i * real, row, col).reshape(shape)
        return carry

    lax.fori_loop(0, slots, one, 0)

    out_order = [flipped_by(z, SPREAD - 1 - t) for t in range(SPREAD)]
    bits = [bit_of(region if axis == "region" else dev, w) for axis, w in plan.scatter]
    offsets = [0]
    for bit, size in zip(bits, plan.sizes[1:]):
        offsets.append(offsets[-1] + bit * size)

    def core_copy(t):
        j = out_order[t]
        return remote(grad.at[1 - core, j], halved.at[j], core_sem.at[0, t], core_sem.at[1, t], sibling)

    def pair_copy(i, t):
        j, size = out_order[t], plan.sizes[i + 1]
        src = whole if i == 0 else held[i - 1]
        rows = pl.ds(pl.multiple_of((1 - bits[i]) * size, TILE), size)
        return remote(
            src.at[j, rows, :], came[i].at[j], pair_sem.at[0, i, t], pair_sem.at[1, i, t], partner(plan.scatter[i])
        )

    last = held[-1] if plan.scatter else whole

    def z_copy(t):
        j = out_order[t]
        return remote(last.at[j], final.at[z], z_sem.at[0, t], z_sem.at[1, t], across(j))

    for t in range(SPREAD):
        core_copy(t).start()

    def strip(s, carry):
        start = pl.multiple_of(s * STRIP, STRIP)
        rows = pl.ds(start, STRIP)
        at = start + lax.broadcasted_iota(jnp.int32, (STRIP, frame), 0)
        across_at = lax.broadcasted_iota(jnp.int32, (STRIP, frame), 1)
        sums = [jnp.zeros((STRIP, frame), jnp.float32) for _ in range(8)]
        for k in range(slots):
            row, col = rows_s[k], cols_s[k]
            p_r, p_i = rolled[k, 0, rows, :], rolled[k, 1, rows, :]
            b_r, b_i = back[k, 0, rows, :], back[k, 1, rows, :]
            own, low = at >= row, across_at >= col
            for plane, x in enumerate((p_r * b_r + p_i * b_i, p_r * b_i - p_i * b_r)):
                mine, next_ = jnp.where(own, x, 0.0), jnp.where(own, 0.0, x)
                for side, y in enumerate((mine, next_)):
                    at_ = 4 * plane + 2 * side
                    sums[at_] = sums[at_] + jnp.where(low, y, 0.0)
                    sums[at_ + 1] = sums[at_ + 1] + jnp.where(low, 0.0, y)
        for plane in (0, 1):
            for side, ref in enumerate((total, ahead)):
                for part in (0, 1):
                    ref[plane, rows, part * frame:(part + 1) * frame] = sums[4 * plane + 2 * side + part]
        return carry

    per = step // STRIP
    for c in range(CHUNKS):
        lax.fori_loop(c * per, (c + 1) * per, strip, 0)

        @pl.when(has_next)
        def _():
            total_copy(c).start()

    for t in range(SPREAD):
        core_copy(t).wait_recv()
        j = out_order[t]
        whole[j] = grad[core, j] + halved[j]
        if plan.scatter:
            pair_copy(0, t).start()
    for i in range(len(plan.scatter)):
        src = whole if i == 0 else held[i - 1]
        for t in range(SPREAD):
            j, size = out_order[t], plan.sizes[i + 1]
            pair_copy(i, t).wait_recv()
            held[i][j] = src[j, pl.ds(pl.multiple_of(bits[i] * size, TILE), size), :] + came[i][j]
            if i + 1 < len(plan.scatter):
                pair_copy(i + 1, t).start()
            elif t < SPREAD - 1:
                z_copy(t).start()
    mine = last[z]
    for t in range(SPREAD - 1):
        z_copy(t).wait_recv()
    for t in range(SPREAD - 1):
        mine = mine + final[out_order[t]]
    for i in range(len(plan.double)):
        given[i][...] = mine
        copy = remote(given[i], twice[i], double_sem.at[0, i], double_sem.at[1, i], partner(plan.double[i]))
        copy.start()
        copy.wait_recv()
        mine = mine + twice[i][...]

    back_order = [flipped_by(z, t) for t in range(SPREAD)]
    place = pl.ds(pl.multiple_of(offsets[-1], TILE), plan.piece)
    gathered[core, z, place, :] = mine

    def zback_copy(t):
        ref = gathered.at[core, z, place, :]
        return remote(ref, ref, zback_sem.at[0, t], zback_sem.at[1, t], across(back_order[t]))

    def pback_copy(i, t):
        rows = pl.ds(pl.multiple_of(offsets[i + 1], TILE), plan.sizes[i + 1])
        ref = gathered.at[core, back_order[t], rows, :]
        return remote(ref, ref, pback_sem.at[0, i, t], pback_sem.at[1, i, t], partner(plan.scatter[i]))

    def cback_copy(t):
        ref = gathered.at[core, back_order[t]]
        return remote(ref, ref, cback_sem.at[0, t], cback_sem.at[1, t], sibling)

    for t in range(1, SPREAD):
        zback_copy(t).start()
    depth = len(plan.scatter)
    for s in range(SPREAD + depth + 1):
        for level in range(depth + 2):
            t = s - level
            if not 0 <= t < SPREAD:
                continue
            if level == 0:
                if t:
                    zback_copy(t).wait_recv()
            elif level <= depth:
                pback_copy(depth - level, t).wait_recv()
            else:
                cback_copy(t).wait_recv()
            if level < depth:
                pback_copy(depth - 1 - level, t).start()
            elif level == depth:
                cback_copy(t).start()

    summed = gathered[...].reshape(probe.shape)
    step_scale = 0.25 * lax.rsqrt(jnp.sum(summed * summed) / summed.size + 1e-06)
    new_probe[...] = probe[...] - step_scale * summed

    for c in range(CHUNKS):
        @pl.when(has_prior)
        def _():
            total_copy(c).wait_recv()

        rows = pl.ds(c * step, step)
        bottom = 1.0 / (weight[rows, :] + 1.0)
        for plane in (0, 1):
            new_field[plane, rows, :] = field[plane, rows, :] - (total[plane, rows, :] + arrived[plane, rows, :]) * bottom

    @pl.when(has_prior)
    def _():
        for c in range(CHUNKS):
            rim_copy(c).wait_send()

    @pl.when(has_next)
    def _():
        for i in range(3):
            prior_copy(i).wait_send()
        for c in range(CHUNKS):
            total_copy(c).wait_send()

    for t in range(SPREAD):
        core_copy(t).wait_send()
        cback_copy(t).wait_send()
        for i in range(depth):
            pair_copy(i, t).wait_send()
            pback_copy(i, t).wait_send()
        if t < SPREAD - 1:
            z_copy(t).wait_send()
        if t:
            zback_copy(t).wait_send()
    for i in range(len(plan.double)):
        remote(given[i], twice[i], double_sem.at[0, i], double_sem.at[1, i], partner(plan.double[i])).wait_send()


def on_device(plan, object_field, probe, amplitudes, row_offset, col_offset, frame_count):
    _, band, width = object_field.shape
    frame = probe.shape[1]
    slots = amplitudes.shape[2]
    smem = pl.BlockSpec(memory_space=pltpu.SMEM)
    anywhere = pl.BlockSpec(memory_space=pl.ANY)
    vmem = pl.BlockSpec(memory_space=pltpu.VMEM)

    def floats(*shape):
        return pltpu.VMEM(shape, jnp.float32)

    def sems(*shape):
        return pltpu.SemaphoreType.DMA(shape)

    tables = fourier_tables(frame)
    levels, doubles = max(1, len(plan.scatter)), max(1, len(plan.double))
    scratch = [
        pltpu.SMEM((slots,), jnp.int32), pltpu.SMEM((slots,), jnp.int32), pltpu.SMEM((1,), jnp.int32),
        floats(2, band, width), floats(2, band, width), floats(2, frame, frame), floats(slots, frame, frame),
        pltpu.VMEM(tables.shape, jnp.bfloat16),
        floats(slots, 2, frame, frame), floats(slots, 2, frame, frame), floats(slots, frame, frame),
        floats(slots, 2, frame, frame), floats(slots, 2, frame, frame),
        pltpu.VMEM((2, slots * (band // CHUNKS), 3 * frame), jnp.bfloat16),
        floats(band, width), floats(2, band, width), floats(2, band, width), floats(2, band, width),
        floats(2, SPREAD, plan.rows, frame), floats(SPREAD, plan.rows, frame), floats(SPREAD, plan.rows, frame),
        floats(SPREAD, plan.piece, frame), floats(2, SPREAD, plan.rows, frame),
    ]
    scratch += [floats(SPREAD, size, frame) for size in plan.sizes[1:]] * 2
    scratch += [floats(plan.piece, frame) for _ in plan.double] * 2
    scratch += [
        sems(4), sems(2, CHUNKS), sems(2, 3), sems(2, CHUNKS), sems(2, SPREAD), sems(2, levels, SPREAD),
        sems(2, SPREAD), sems(2, doubles), sems(2, SPREAD), sems(2, levels, SPREAD), sems(2, SPREAD),
    ]
    return pl.pallas_call(
        functools.partial(kernel, plan),
        out_shape=(
            jax.ShapeDtypeStruct(object_field.shape, jnp.float32),
            jax.ShapeDtypeStruct(probe.shape, jnp.float32),
        ),
        in_specs=[smem] * 3 + [anywhere] * 4,
        out_specs=(vmem,) * 2,
        scratch_shapes=scratch,
        compiler_params=pltpu.CompilerParams(
            collective_id=0, has_side_effects=True, vmem_limit_bytes=60 * 1024 * 1024
        ),
    )(row_offset[0, 0], col_offset[0, 0], frame_count[0], object_field, probe, amplitudes[0, 0], tables)


def solution(mesh):
    def step(*args):
        plan = Plan(mesh.shape["region"], mesh.shape["dev"], args[1].shape[1])
        return on_device(plan, *args)

    return jax.shard_map(
        step,
        mesh=mesh,
        in_specs=(
            P(None, ("region", "dev"), None),
            P(),
            P("region", "dev", None, None, None),
            P("region", "dev", None),
            P("region", "dev", None),
            P("region", "dev"),
        ),
        out_specs=(P(None, ("region", "dev"), None), P()),
        check_vma=False,
    )
```

time: 97.7 us -> 63.4 us (0.65)
  the two profiles are of different devices: /device:TPU:16 before, /device:TPU:1 now
where the time goes in v1:
time: 63.4 us; the launch traced here: 63.2 us
  Pallas kernels  58.8 us (93%)
  local copies, waits for them, and re-layouts  3.12 us (5%)
  between operations  1.29 us (2%)
    pallas_call x1, Pallas kernels, on_device(): pl.pallas_call(functools.partial(kernel, plan), out_shape=(jax.ShapeDtype...  58.8 us
    unnamed x4, local copies, waits for them, and re-layouts  3.12 us

profile of v1, /device:TPU:1, one launch (start us, length us, event | category | flops | bytes accessed | tf_op | source)
XLA Modules:
  0.0 63.2 jit_solution(16378013260243508509)
XLA Ops:
  1.3 58.8 %shard_map.86 = (f32[2,256,512]{2,1,0:T(8,128)}, f32[2,256,256]{2,1,0:T(8,128)}) custom-call(s32[4]{0:T(128)} %bitcast.6, s32[4]{0:T(128)} %bitcast.7, s32[1]{0:T(128)} %bitcast.4.count_s, f32[2,256,512]{2,1,0:T(8,128)} %field_h.1, f32[2,256,256]{2,1,0:T(8,128)} %probe_h.1, f32[4,256,256]{2,1,0:T(8,128)} %bitcast.5, ...), custom_call_target="tpu_custom_call" | custom-call | tf_op jit(solution)/shard_map/pallas_call | solution.py:519
  60.1 0.0 copy-start
  60.1 2.3 %copy.12 = f32[2,256,512]{2,1,0:T(8,128)} copy(f32[2,256,512]{2,1,0:T(8,128)} %get-tuple-element.4) | data formatting | bytes 2097152
  62.4 0.0 copy-done
  62.4 0.8 %copy.13 = f32[2,256,256]{2,1,0:T(8,128)} copy(f32[2,256,256]{2,1,0:T(8,128)S(1)} %copy-done) | data formatting | bytes 1048576
Async XLA Ops:
  60.1 2.3 %copy-start = (f32[2,256,256]{2,1,0:T(8,128)S(1)}, f32[2,256,256]{2,1,0:T(8,128)}, u32[]{:S(2)}) copy-start(f32[2,256,256]{2,1,0:T(8,128)} %get-tuple-element.5) | copy-start | bytes 1572868

commit v2 on v1

--- a/solution.py
+++ b/solution.py
@@ -14,6 +14,9 @@
 TILE = 8
 CHUNKS = 4
 STRIP = 16
+TOTALS = 16
+VMEM = 30 * 1024 * 1024
+PACE = (3, 1, 1, 3, 1, 1)
 
 
 def halves(x):
@@ -88,18 +91,17 @@
         pairs += [("dev", 1 << b) for b in range(1, self.stride.bit_length() - 1)]
         most = (self.rows // TILE).bit_length() - 1
         self.scatter, self.double = pairs[:most], pairs[most:]
-        self.sizes = [self.rows >> i for i in range(len(self.scatter) + 1)]
-        self.piece = self.sizes[-1]
-
-
-def kernel(plan, rows_s, cols_s, count_s, field_h, probe_h, amps_h, tables_h, new_field, new_probe, *scratch):
+        self.piece = self.rows >> len(self.scatter)
+        self.others = (1 << len(self.scatter)) - 1
+
+
+def kernel(plan, rows_h, cols_h, count_h, field_h, probe_h, amps_h, tables_h, new_field, new_probe, *scratch):
     (
-        prior_rows, prior_cols, prior_count, field, rim, probe, amps, tables, rolled, window, wanted, spec, back,
+        rows_s, cols_s, count_s, prior_rows, prior_cols, prior_count, field, rim, probe, amps, tables, rolled, window, wanted, spec, back,
         left_side, weight, total, ahead, arrived, grad, halved, whole, final, gathered,
-    ) = scratch[:23]
-    rest = list(scratch[23:])
-    came = [rest.pop(0) for _ in plan.scatter]
-    held = [rest.pop(0) for _ in plan.scatter]
+    ) = scratch[:26]
+    rest = list(scratch[26:])
+    came, held = rest.pop(0), rest.pop(0)
     twice = [rest.pop(0) for _ in plan.double]
     given = [rest.pop(0) for _ in plan.double]
     local, rim_sem, prior_sem, total_sem, core_sem, pair_sem, z_sem, double_sem, zback_sem, pback_sem, cback_sem = rest
@@ -120,16 +122,35 @@
     def across(other):
         return (region, lax.rem(dev, plan.stride) + other * plan.stride)
 
+    masks = range(1, 1 << len(plan.scatter))
+
+    def member(mask):
+        where = (region, dev)
+        for i, (axis, weight_) in enumerate(plan.scatter):
+            if mask >> i & 1:
+                at = ("region", "dev").index(axis)
+                where = where[:at] + (flipped(where[at], weight_),) + where[at + 1:]
+        return where
+
+    def block_of(where):
+        block = 0
+        for i, (axis, weight_) in enumerate(plan.scatter):
+            block = block + bit_of(where[("region", "dev").index(axis)], weight_) * (1 << i)
+        return pl.ds(pl.multiple_of(block * plan.piece, TILE), plan.piece)
+
     sibling = partner(("dev", 1))
     behind = (region, lax.rem(dev + devs - 1, devs))
     beyond = (region, lax.rem(dev + 1, devs))
 
     loads = []
-    for i, (src, dst) in enumerate(((probe_h, probe), (field_h, field), (amps_h, amps), (tables_h, tables))):
+    for i, (src, dst) in enumerate((
+        (probe_h, probe), (field_h, field), (amps_h, amps), (tables_h, tables),
+        (rows_h, rows_s), (cols_h, cols_s), (count_h, count_s),
+    )):
         loads.append(pltpu.make_async_copy(src, dst, local.at[i]))
         loads[-1].start()
 
-    peers = [sibling, behind, beyond] + [partner(p) for p in plan.scatter + plan.double]
+    peers = [sibling, behind, beyond] + [member(mask) for mask in masks] + [partner(p) for p in plan.double]
     peers += [across(flipped_by(z, t)) for t in range(1, SPREAD)]
     barrier = pltpu.get_barrier_semaphore()
     for peer in peers:
@@ -143,12 +164,12 @@
         return remote(field_h.at[:, rows, :], rim.at[:, rows, :], rim_sem.at[0, c], rim_sem.at[1, c], behind)
 
     def prior_copy(i):
-        src = (rows_s, cols_s, count_s)[i]
+        src = (rows_h, cols_h, count_h)[i]
         dst = (prior_rows, prior_cols, prior_count)[i]
         return remote(src, dst, prior_sem.at[0, i], prior_sem.at[1, i], beyond)
 
     def total_copy(c):
-        rows = pl.ds(c * step, step)
+        rows = pl.ds(c * (band // TOTALS), band // TOTALS)
         return remote(ahead.at[:, rows, :], arrived.at[:, rows, :], total_sem.at[0, c], total_sem.at[1, c], beyond)
 
     has_next, has_prior = dev < devs - 1, dev > 0
@@ -171,9 +192,9 @@
     def _():
         arrived[...] = jnp.zeros_like(arrived)
         for i in range(slots):
-            prior_rows[i] = 0
-            prior_cols[i] = 0
-        prior_count[0] = 0
+            prior_rows[0, 0, i] = 0
+            prior_cols[0, 0, i] = 0
+        prior_count[0, 0] = 0
 
     row_at = lax.broadcasted_iota(jnp.int32, (frame, frame), 0)
     col_at = lax.broadcasted_iota(jnp.int32, (frame, frame), 1)
@@ -188,15 +209,16 @@
         x = pltpu.roll(x, lax.rem(2 * frame - col, frame), 1)
         return pltpu.roll(x, lax.rem(frame - row, frame), 0)
 
-    loads[0].wait()
+    for i in (0, 4, 5, 6):
+        loads[i].wait()
     weight[...] = jnp.zeros_like(weight)
 
     def prepare(k, carry):
-        row, col = rows_s[k], cols_s[k]
+        row, col = rows_s[0, 0, k], cols_s[0, 0, k]
         real, imag = turned(probe[0], row, col), turned(probe[1], row, col)
         rolled[k, 0] = real
         rolled[k, 1] = imag
-        power = (real * real + imag * imag) * live(k, count_s[0])
+        power = (real * real + imag * imag) * live(k, count_s[0, 0])
         power = jnp.where(row_at >= row, power, 0.0)
         weight[:, :frame] += jnp.where(col_at >= col, power, 0.0)
         weight[:, frame:] += jnp.where(col_at >= col, 0.0, power)
@@ -234,9 +256,9 @@
             prior_copy(i).wait_recv()
 
     def prior(k, carry):
-        row, col = prior_rows[k], prior_cols[k]
+        row, col = prior_rows[0, 0, k], prior_cols[0, 0, k]
         power = probe[0] * probe[0] + probe[1] * probe[1]
-        power = turned(power, row, col) * live(k, prior_count[0])
+        power = turned(power, row, col) * live(k, prior_count[0, 0])
         power = jnp.where(row_at < row, power, 0.0)
         weight[:, :frame] += jnp.where(col_at >= col, power, 0.0)
         weight[:, frame:] += jnp.where(col_at >= col, 0.0, power)
@@ -255,7 +277,7 @@
         rows = pl.ds(start, step)
         at = start + lax.broadcasted_iota(jnp.int32, (step, width), 0)
         for k in range(slots):
-            row, col = rows_s[k], cols_s[k]
+            row, col = rows_s[0, 0, k], cols_s[0, 0, k]
             pieces = []
             for plane in (0, 1):
                 x = jnp.where(at >= row, field[plane, rows, :], rim[plane, rows, :])
@@ -305,14 +327,14 @@
         imag = jnp.concatenate([add[half:], sub[half:]], axis=0)
         even = times_right(jnp.concatenate([real[:, :half], imag[:, :half]], axis=1), tables, 2)
         odd = times_right(jnp.concatenate([real[:, half:], imag[:, half:]], axis=1), tables, 3)
-        alive = live(k, count_s[0])
+        alive = live(k, count_s[0, 0])
         add, sub = (even + odd) * alive, (even - odd) * alive
         real = jnp.concatenate([add[:, :half], sub[:, :half]], axis=1)
         imag = jnp.concatenate([add[:, half:], sub[:, half:]], axis=1)
         back[k, 0] = real
         back[k, 1] = imag
         w_r, w_i = window[k, 0], window[k, 1]
-        row, col = rows_s[k], cols_s[k]
+        row, col = rows_s[0, 0, k], cols_s[0, 0, k]
         shape = grad.shape[1:]
         grad[0] += turned_back(w_r * real + w_i * imag, row, col).reshape(shape)
         grad[1] += turned_back(w_r * imag - w_i * real, row, col).reshape(shape)
@@ -321,28 +343,29 @@
     lax.fori_loop(0, slots, one, 0)
 
     out_order = [flipped_by(z, SPREAD - 1 - t) for t in range(SPREAD)]
-    bits = [bit_of(region if axis == "region" else dev, w) for axis, w in plan.scatter]
-    offsets = [0]
-    for bit, size in zip(bits, plan.sizes[1:]):
-        offsets.append(offsets[-1] + bit * size)
-
     def core_copy(t):
         j = out_order[t]
         return remote(grad.at[1 - core, j], halved.at[j], core_sem.at[0, t], core_sem.at[1, t], sibling)
 
-    def pair_copy(i, t):
-        j, size = out_order[t], plan.sizes[i + 1]
-        src = whole if i == 0 else held[i - 1]
-        rows = pl.ds(pl.multiple_of((1 - bits[i]) * size, TILE), size)
+    def group_copy(t, mask):
+        j, peer = out_order[t], member(mask)
         return remote(
-            src.at[j, rows, :], came[i].at[j], pair_sem.at[0, i, t], pair_sem.at[1, i, t], partner(plan.scatter[i])
+            whole.at[j, block_of(peer), :], came.at[j, mask - 1],
+            pair_sem.at[0, t, mask - 1], pair_sem.at[1, t, mask - 1], peer,
         )
-
-    last = held[-1] if plan.scatter else whole
 
     def z_copy(t):
         j = out_order[t]
-        return remote(last.at[j], final.at[z], z_sem.at[0, t], z_sem.at[1, t], across(j))
+        return remote(held.at[j], final.at[z], z_sem.at[0, t], z_sem.at[1, t], across(j))
+
+    sent = [0]
+
+    def send_totals(count):
+        for c in range(sent[0], min(sent[0] + count, TOTALS)):
+            @pl.when(has_next)
+            def _():
+                total_copy(c).start()
+        sent[0] += count
 
     for t in range(SPREAD):
         core_copy(t).start()
@@ -354,7 +377,7 @@
         across_at = lax.broadcasted_iota(jnp.int32, (STRIP, frame), 1)
         sums = [jnp.zeros((STRIP, frame), jnp.float32) for _ in range(8)]
         for k in range(slots):
-            row, col = rows_s[k], cols_s[k]
+            row, col = rows_s[0, 0, k], cols_s[0, 0, k]
             p_r, p_i = rolled[k, 0, rows, :], rolled[k, 1, rows, :]
             b_r, b_i = back[k, 0, rows, :], back[k, 1, rows, :]
             own, low = at >= row, across_at >= col
@@ -370,31 +393,28 @@
                     ref[plane, rows, part * frame:(part + 1) * frame] = sums[4 * plane + 2 * side + part]
         return carry
 
-    per = step // STRIP
-    for c in range(CHUNKS):
-        lax.fori_loop(c * per, (c + 1) * per, strip, 0)
-
-        @pl.when(has_next)
-        def _():
-            total_copy(c).start()
-
+    lax.fori_loop(0, band // STRIP, strip, 0)
+
+    mine_at = block_of((region, dev))
     for t in range(SPREAD):
         core_copy(t).wait_recv()
         j = out_order[t]
         whole[j] = grad[core, j] + halved[j]
-        if plan.scatter:
-            pair_copy(0, t).start()
-    for i in range(len(plan.scatter)):
-        src = whole if i == 0 else held[i - 1]
-        for t in range(SPREAD):
-            j, size = out_order[t], plan.sizes[i + 1]
-            pair_copy(i, t).wait_recv()
-            held[i][j] = src[j, pl.ds(pl.multiple_of(bits[i] * size, TILE), size), :] + came[i][j]
-            if i + 1 < len(plan.scatter):
-                pair_copy(i + 1, t).start()
-            elif t < SPREAD - 1:
-                z_copy(t).start()
-    mine = last[z]
+        for mask in masks:
+            group_copy(t, mask).start()
+    send_totals(PACE[0])
+    for t in range(SPREAD):
+        j = out_order[t]
+        acc = whole[j, mine_at, :]
+        for mask in masks:
+            group_copy(t, mask).wait_recv()
+            acc = acc + came[j, mask - 1]
+        if t < SPREAD - 1:
+            held[j] = acc
+            z_copy(t).start()
+            send_totals(PACE[1])
+    mine = acc
+    send_totals(PACE[2])
     for t in range(SPREAD - 1):
         z_copy(t).wait_recv()
     for t in range(SPREAD - 1):
@@ -407,17 +427,15 @@
         mine = mine + twice[i][...]
 
     back_order = [flipped_by(z, t) for t in range(SPREAD)]
-    place = pl.ds(pl.multiple_of(offsets[-1], TILE), plan.piece)
-    gathered[core, z, place, :] = mine
+    gathered[core, z, mine_at, :] = mine
 
     def zback_copy(t):
-        ref = gathered.at[core, z, place, :]
+        ref = gathered.at[core, z, mine_at, :]
         return remote(ref, ref, zback_sem.at[0, t], zback_sem.at[1, t], across(back_order[t]))
 
-    def pback_copy(i, t):
-        rows = pl.ds(pl.multiple_of(offsets[i + 1], TILE), plan.sizes[i + 1])
-        ref = gathered.at[core, back_order[t], rows, :]
-        return remote(ref, ref, pback_sem.at[0, i, t], pback_sem.at[1, i, t], partner(plan.scatter[i]))
+    def gback_copy(t, mask):
+        ref = gathered.at[core, back_order[t], mine_at, :]
+        return remote(ref, ref, pback_sem.at[0, t, mask - 1], pback_sem.at[1, t, mask - 1], member(mask))
 
     def cback_copy(t):
         ref = gathered.at[core, back_order[t]]
@@ -425,32 +443,33 @@
 
     for t in range(1, SPREAD):
         zback_copy(t).start()
-    depth = len(plan.scatter)
-    for s in range(SPREAD + depth + 1):
-        for level in range(depth + 2):
-            t = s - level
-            if not 0 <= t < SPREAD:
-                continue
-            if level == 0:
-                if t:
-                    zback_copy(t).wait_recv()
-            elif level <= depth:
-                pback_copy(depth - level, t).wait_recv()
-            else:
-                cback_copy(t).wait_recv()
-            if level < depth:
-                pback_copy(depth - 1 - level, t).start()
-            elif level == depth:
-                cback_copy(t).start()
+    for mask in masks:
+        gback_copy(0, mask).start()
+    send_totals(PACE[3])
+    for t in range(1, SPREAD):
+        zback_copy(t).wait_recv()
+        for mask in masks:
+            gback_copy(t, mask).start()
+        send_totals(PACE[4])
+    for t in range(SPREAD):
+        for mask in masks:
+            gback_copy(t, mask).wait_recv()
+        cback_copy(t).start()
+        send_totals(PACE[5])
+    for t in range(SPREAD):
+        cback_copy(t).wait_recv()
+    send_totals(TOTALS)
 
     summed = gathered[...].reshape(probe.shape)
     step_scale = 0.25 * lax.rsqrt(jnp.sum(summed * summed) / summed.size + 1e-06)
     new_probe[...] = probe[...] - step_scale * summed
 
+    share = TOTALS // CHUNKS
     for c in range(CHUNKS):
         @pl.when(has_prior)
         def _():
-            total_copy(c).wait_recv()
+            for i in range(share):
+                total_copy(c * share + i).wait_recv()
 
         rows = pl.ds(c * step, step)
         bottom = 1.0 / (weight[rows, :] + 1.0)
@@ -466,15 +485,15 @@
     def _():
         for i in range(3):
             prior_copy(i).wait_send()
-        for c in range(CHUNKS):
+        for c in range(TOTALS):
             total_copy(c).wait_send()
 
     for t in range(SPREAD):
         core_copy(t).wait_send()
         cback_copy(t).wait_send()
-        for i in range(depth):
-            pair_copy(i, t).wait_send()
-            pback_copy(i, t).wait_send()
+        for mask in masks:
+            group_copy(t, mask).wait_send()
+            gback_copy(t, mask).wait_send()
         if t < SPREAD - 1:
             z_copy(t).wait_send()
         if t:
@@ -487,8 +506,7 @@
     _, band, width = object_field.shape
     frame = probe.shape[1]
     slots = amplitudes.shape[2]
-    smem = pl.BlockSpec(memory_space=pltpu.SMEM)
-    anywhere = pl.BlockSpec(memory_space=pl.ANY)
+    hbm = pl.BlockSpec(memory_space=pltpu.HBM)
     vmem = pl.BlockSpec(memory_space=pltpu.VMEM)
 
     def floats(*shape):
@@ -498,9 +516,10 @@
         return pltpu.SemaphoreType.DMA(shape)
 
     tables = fourier_tables(frame)
-    levels, doubles = max(1, len(plan.scatter)), max(1, len(plan.double))
+    operands = (row_offset, col_offset, frame_count, object_field, probe, amplitudes[0, 0], tables)
+    doubles = max(1, len(plan.double))
     scratch = [
-        pltpu.SMEM((slots,), jnp.int32), pltpu.SMEM((slots,), jnp.int32), pltpu.SMEM((1,), jnp.int32),
+        *[pltpu.SMEM(x.shape, jnp.int32) for x in (row_offset, col_offset, frame_count)] * 2,
         floats(2, band, width), floats(2, band, width), floats(2, frame, frame), floats(slots, frame, frame),
         pltpu.VMEM(tables.shape, jnp.bfloat16),
         floats(slots, 2, frame, frame), floats(slots, 2, frame, frame), floats(slots, frame, frame),
@@ -510,11 +529,11 @@
         floats(2, SPREAD, plan.rows, frame), floats(SPREAD, plan.rows, frame), floats(SPREAD, plan.rows, frame),
         floats(SPREAD, plan.piece, frame), floats(2, SPREAD, plan.rows, frame),
     ]
-    scratch += [floats(SPREAD, size, frame) for size in plan.sizes[1:]] * 2
+    scratch += [floats(SPREAD, plan.others, plan.piece, frame), floats(SPREAD, plan.piece, frame)]
     scratch += [floats(plan.piece, frame) for _ in plan.double] * 2
     scratch += [
-        sems(4), sems(2, CHUNKS), sems(2, 3), sems(2, CHUNKS), sems(2, SPREAD), sems(2, levels, SPREAD),
-        sems(2, SPREAD), sems(2, doubles), sems(2, SPREAD), sems(2, levels, SPREAD), sems(2, SPREAD),
+        sems(7), sems(2, CHUNKS), sems(2, 3), sems(2, TOTALS), sems(2, SPREAD), sems(2, SPREAD, plan.others),
+        sems(2, SPREAD), sems(2, doubles), sems(2, SPREAD), sems(2, SPREAD, plan.others), sems(2, SPREAD),
     ]
     return pl.pallas_call(
         functools.partial(kernel, plan),
@@ -522,13 +541,13 @@
             jax.ShapeDtypeStruct(object_field.shape, jnp.float32),
             jax.ShapeDtypeStruct(probe.shape, jnp.float32),
         ),
-        in_specs=[smem] * 3 + [anywhere] * 4,
+        in_specs=[hbm, hbm, pl.BlockSpec(memory_space=pl.ANY)] + [hbm] * 4,
         out_specs=(vmem,) * 2,
         scratch_shapes=scratch,
         compiler_params=pltpu.CompilerParams(
-            collective_id=0, has_side_effects=True, vmem_limit_bytes=60 * 1024 * 1024
+            collective_id=0, has_side_effects=True, vmem_limit_bytes=VMEM
         ),
-    )(row_offset[0, 0], col_offset[0, 0], frame_count[0], object_field, probe, amplitudes[0, 0], tables)
+    )(*[x if x is frame_count else pltpu.with_memory_space_constraint(x, pltpu.HBM) for x in operands])
 
 
 def solution(mesh):

time: 63.4 us -> 51.9 us (0.82)
  Pallas kernels: 58.8 us -> 48.7 us
  local copies, waits for them, and re-layouts: 3.12 us -> 1.77 us
    pallas_call x1, Pallas kernels: 58.8 us -> 48.7 us  [on_device(): pl.pallas_call(functools.partial(kernel, plan), out_shape=(jax.ShapeDtype...]
    unnamed x4 -> x2, local copies, waits for them, and re-layouts: 3.12 us -> 1.77 us
where the time goes in v2:
time: 51.9 us; the launch traced here: 51.8 us
  Pallas kernels  48.7 us (94%)
  local copies, waits for them, and re-layouts  1.77 us (3%)
  between operations  1.29 us (2%)
    pallas_call x1, Pallas kernels, on_device(): pl.pallas_call(functools.partial(kernel, plan), out_shape=(jax.ShapeDtype...  48.7 us
    unnamed x2, local copies, waits for them, and re-layouts  1.77 us

profile of v2, /device:TPU:1, one launch (start us, length us, event | category | flops | bytes accessed | tf_op | source)
XLA Modules:
  0.0 51.8 jit_solution(10217190409414483893)
XLA Ops:
  1.3 48.7 %shard_map.86 = (f32[2,256,512]{2,1,0:T(8,128)S(1)}, f32[2,256,256]{2,1,0:T(8,128)S(1)}) custom-call(s32[1,1,4]{2,1,0:T(1,128)} %rows_h.1, s32[1,1,4]{2,1,0:T(1,128)} %cols_h.1, s32[1,1]{1,0:T(1,128)S(6)} %copy.11.count_h, f32[2,256,512]{2,1,0:T(8,128)} %field_h.1, f32[2,256,256]{2,1,0:T(8,128)} %probe_h.1, f32[4,256,256]{2,1,0:T(8,128)} %bitcast.1, ...), custom_call_target="tpu_custom_call" | custom-call | tf_op jit(solution)/shard_map/pallas_call | solution.py:538
  50.0 1.0 %copy.12 = f32[2,256,512]{2,1,0:T(8,128)} copy(f32[2,256,512]{2,1,0:T(8,128)S(1)} %get-tuple-element.4) | data formatting | bytes 2097152
  51.0 0.8 %copy.13 = f32[2,256,256]{2,1,0:T(8,128)} copy(f32[2,256,256]{2,1,0:T(8,128)S(1)} %get-tuple-element.5) | data formatting | bytes 1048576

commit v3 on v2

--- a/solution.py
+++ b/solution.py
@@ -15,6 +15,8 @@
 CHUNKS = 4
 STRIP = 16
 TOTALS = 16
+UPDATES = 4
+EARLY = (0, 2)
 VMEM = 30 * 1024 * 1024
 PACE = (3, 1, 1, 3, 1, 1)
 
@@ -85,14 +87,15 @@
 class Plan:
     def __init__(self, regions, devs, frame):
         self.regions, self.devs = regions, devs
-        self.stride = devs // SPREAD
         self.rows = frame // SPREAD
+        self.far = [("dev", 2), ("dev", devs // 2)]
         pairs = [("region", 1 << b) for b in range(regions.bit_length() - 1)]
-        pairs += [("dev", 1 << b) for b in range(1, self.stride.bit_length() - 1)]
+        pairs += [("dev", 1 << b) for b in range(2, devs.bit_length() - 2)]
         most = (self.rows // TILE).bit_length() - 1
         self.scatter, self.double = pairs[:most], pairs[most:]
         self.piece = self.rows >> len(self.scatter)
         self.others = (1 << len(self.scatter)) - 1
+        self.levels = max(len(self.scatter), 2) - 1
 
 
 def kernel(plan, rows_h, cols_h, count_h, field_h, probe_h, amps_h, tables_h, new_field, new_probe, *scratch):
@@ -104,14 +107,14 @@
     came, held = rest.pop(0), rest.pop(0)
     twice = [rest.pop(0) for _ in plan.double]
     given = [rest.pop(0) for _ in plan.double]
-    local, rim_sem, prior_sem, total_sem, core_sem, pair_sem, z_sem, double_sem, zback_sem, pback_sem, cback_sem = rest
+    local, rim_sem, prior_sem, total_sem, core_sem, pair_sem, z_sem, double_sem, zback_sem, pback_sem, cback_sem, ready = rest
     region, dev = lax.axis_index("region"), lax.axis_index("dev")
     devs = plan.devs
     slots, frame = amps.shape[0], probe.shape[1]
     half = frame // 2
     band = field.shape[1]
     core = lax.rem(dev, 2)
-    z = lax.div(dev, plan.stride)
+    z = bit_of(dev, plan.far[0][1]) + 2 * bit_of(dev, plan.far[1][1])
 
     def partner(pair):
         axis, weight_ = pair
@@ -119,8 +122,12 @@
             return (flipped(region, weight_), dev)
         return (region, flipped(dev, weight_))
 
-    def across(other):
-        return (region, lax.rem(dev, plan.stride) + other * plan.stride)
+    def across(number):
+        other = dev
+        for i, (_, weight_) in enumerate(plan.far):
+            if number >> i & 1:
+                other = flipped(other, weight_)
+        return (region, other)
 
     masks = range(1, 1 << len(plan.scatter))
 
@@ -150,12 +157,18 @@
         loads.append(pltpu.make_async_copy(src, dst, local.at[i]))
         loads[-1].start()
 
-    peers = [sibling, behind, beyond] + [member(mask) for mask in masks] + [partner(p) for p in plan.double]
-    peers += [across(flipped_by(z, t)) for t in range(1, SPREAD)]
+    has_next, has_prior = dev < devs - 1, dev > 0
+    near = [partner(pair) for pair in plan.scatter + plan.double + plan.far]
     barrier = pltpu.get_barrier_semaphore()
-    for peer in peers:
-        pl.semaphore_signal(barrier, inc=1, device_id=peer, device_id_type=MESH)
-    pl.semaphore_wait(barrier, len(peers))
+
+    def greet(sem, peer):
+        pl.semaphore_signal(sem, inc=1, device_id=peer, device_id_type=MESH)
+
+    for peer in [sibling] + near:
+        greet(barrier, peer)
+    pl.when(has_prior)(lambda: greet(barrier, behind))
+    pl.when(has_next)(lambda: greet(barrier, beyond))
+    pl.semaphore_wait(barrier, 1 + len(near) + has_prior.astype(jnp.int32) + has_next.astype(jnp.int32))
 
     step = band // CHUNKS
 
@@ -172,7 +185,6 @@
         rows = pl.ds(c * (band // TOTALS), band // TOTALS)
         return remote(ahead.at[:, rows, :], arrived.at[:, rows, :], total_sem.at[0, c], total_sem.at[1, c], beyond)
 
-    has_next, has_prior = dev < devs - 1, dev > 0
 
     @pl.when(has_prior)
     def _():
@@ -183,6 +195,9 @@
     def _():
         for i in range(3):
             prior_copy(i).start()
+
+    for peer in near:
+        greet(ready.at[0], peer)
 
     @pl.when(dev == devs - 1)
     def _():
@@ -340,9 +355,15 @@
         grad[1] += turned_back(w_r * imag - w_i * real, row, col).reshape(shape)
         return carry
 
-    lax.fori_loop(0, slots, one, 0)
+    lax.fori_loop(0, slots, one, 0, unroll=2)
 
     out_order = [flipped_by(z, SPREAD - 1 - t) for t in range(SPREAD)]
+    for level in range(plan.levels):
+        if level:
+            for peer in near:
+                greet(ready.at[level], peer)
+        pl.semaphore_wait(ready.at[level], len(near))
+
     def core_copy(t):
         j = out_order[t]
         return remote(grad.at[1 - core, j], halved.at[j], core_sem.at[0, t], core_sem.at[1, t], sibling)
@@ -356,7 +377,7 @@
 
     def z_copy(t):
         j = out_order[t]
-        return remote(held.at[j], final.at[z], z_sem.at[0, t], z_sem.at[1, t], across(j))
+        return remote(held.at[j], final.at[z], z_sem.at[0, t], z_sem.at[1, t], across(SPREAD - 1 - t))
 
     sent = [0]
 
@@ -431,7 +452,7 @@
 
     def zback_copy(t):
         ref = gathered.at[core, z, mine_at, :]
-        return remote(ref, ref, zback_sem.at[0, t], zback_sem.at[1, t], across(back_order[t]))
+        return remote(ref, ref, zback_sem.at[0, t], zback_sem.at[1, t], across(t))
 
     def gback_copy(t, mask):
         ref = gathered.at[core, back_order[t], mine_at, :]
@@ -451,30 +472,42 @@
         for mask in masks:
             gback_copy(t, mask).start()
         send_totals(PACE[4])
+    share = TOTALS // UPDATES
+    tall = band // UPDATES
+
+    def update(c):
+        @pl.when(has_prior)
+        def _():
+            for i in range(share):
+                total_copy(c * share + i).wait_recv()
+
+        rows = pl.ds(c * tall, tall)
+        bottom = 1.0 / (weight[rows, :] + 1.0)
+        for plane in (0, 1):
+            new_field[plane, rows, :] = field[plane, rows, :] - (total[plane, rows, :] + arrived[plane, rows, :]) * bottom
+
+    def power_of(x):
+        return jnp.sum(x * x)
+
+    for c in range(EARLY[0]):
+        update(c)
     for t in range(SPREAD):
         for mask in masks:
             gback_copy(t, mask).wait_recv()
         cback_copy(t).start()
         send_totals(PACE[5])
+    send_totals(TOTALS)
+    power = power_of(gathered[core])
+    for c in range(EARLY[0], EARLY[1]):
+        update(c)
     for t in range(SPREAD):
         cback_copy(t).wait_recv()
-    send_totals(TOTALS)
-
+    power += power_of(gathered[1 - core])
     summed = gathered[...].reshape(probe.shape)
-    step_scale = 0.25 * lax.rsqrt(jnp.sum(summed * summed) / summed.size + 1e-06)
+    step_scale = 0.25 * lax.rsqrt(power / summed.size + 1e-06)
     new_probe[...] = probe[...] - step_scale * summed
-
-    share = TOTALS // CHUNKS
-    for c in range(CHUNKS):
-        @pl.when(has_prior)
-        def _():
-            for i in range(share):
-                total_copy(c * share + i).wait_recv()
-
-        rows = pl.ds(c * step, step)
-        bottom = 1.0 / (weight[rows, :] + 1.0)
-        for plane in (0, 1):
-            new_field[plane, rows, :] = field[plane, rows, :] - (total[plane, rows, :] + arrived[plane, rows, :]) * bottom
+    for c in range(EARLY[1], UPDATES):
+        update(c)
 
     @pl.when(has_prior)
     def _():
@@ -534,6 +567,7 @@
     scratch += [
         sems(7), sems(2, CHUNKS), sems(2, 3), sems(2, TOTALS), sems(2, SPREAD), sems(2, SPREAD, plan.others),
         sems(2, SPREAD), sems(2, doubles), sems(2, SPREAD), sems(2, SPREAD, plan.others), sems(2, SPREAD),
+        pltpu.SemaphoreType.REGULAR((plan.levels,)),
     ]
     return pl.pallas_call(
         functools.partial(kernel, plan),

time: 51.9 us -> 49.3 us (0.950)
  the two profiles are of different devices: /device:TPU:1 before, /device:TPU:8 now
where the time goes in v3:
time: 49.3 us; the launch traced here: 49.1 us
  Pallas kernels  46.1 us (94%)
  local copies, waits for them, and re-layouts  1.77 us (4%)
  between operations  1.29 us (3%)
    pallas_call x1, Pallas kernels, on_device(): pl.pallas_call(functools.partial(kernel, plan), out_shape=(jax.ShapeDtype...  46.1 us
    unnamed x2, local copies, waits for them, and re-layouts  1.77 us

profile of v3, /device:TPU:8, one launch (start us, length us, event | category | flops | bytes accessed | tf_op | source)
XLA Modules:
  0.0 49.1 jit_solution(7238973662232113208)
XLA Ops:
  1.3 46.1 %shard_map.86 = (f32[2,256,512]{2,1,0:T(8,128)S(1)}, f32[2,256,256]{2,1,0:T(8,128)S(1)}) custom-call(s32[1,1,4]{2,1,0:T(1,128)} %rows_h.1, s32[1,1,4]{2,1,0:T(1,128)} %cols_h.1, s32[1,1]{1,0:T(1,128)S(6)} %copy.11.count_h, f32[2,256,512]{2,1,0:T(8,128)} %field_h.1, f32[2,256,256]{2,1,0:T(8,128)} %probe_h.1, f32[4,256,256]{2,1,0:T(8,128)} %bitcast.1, ...), custom_call_target="tpu_custom_call" | custom-call | tf_op jit(solution)/shard_map/pallas_call | solution.py:572
  47.4 1.0 %copy.12 = f32[2,256,512]{2,1,0:T(8,128)} copy(f32[2,256,512]{2,1,0:T(8,128)S(1)} %get-tuple-element.4) | data formatting | bytes 2097152
  48.4 0.8 %copy.13 = f32[2,256,256]{2,1,0:T(8,128)} copy(f32[2,256,256]{2,1,0:T(8,128)S(1)} %get-tuple-element.5) | data formatting | bytes 1048576

commit v4 on v3

--- a/solution.py
+++ b/solution.py
@@ -16,6 +16,7 @@
 STRIP = 16
 TOTALS = 16
 UPDATES = 4
+TOGETHER = 4
 EARLY = (0, 2)
 VMEM = 30 * 1024 * 1024
 PACE = (3, 1, 1, 3, 1, 1)
@@ -326,36 +327,47 @@
     lax.fori_loop(0, CHUNKS, first, 0)
     grad[...] = jnp.zeros_like(grad)
 
-    def one(k, carry):
-        real, imag = spec[k, 0], spec[k, 1]
+    together = math.gcd(slots, TOGETHER)
+
+    def few(g, carry):
+        ks = [g * together + i for i in range(together)]
+        real = jnp.concatenate([spec[k, 0] for k in ks], axis=1)
+        imag = jnp.concatenate([spec[k, 1] for k in ks], axis=1)
         add = jnp.concatenate([real[:half] + real[half:], imag[:half] + imag[half:]], axis=0)
         sub = jnp.concatenate([real[:half] - real[half:], imag[:half] - imag[half:]], axis=0)
         sides = []
         for i, x in enumerate((add, sub)):
             x = times_left(tables, 2 + i, x)
             real, imag = x[:half], x[half:]
-            factor = 1.0 - wanted[k, i * half:(i + 1) * half, :] * lax.rsqrt(real * real + imag * imag + 0.25)
+            asked = jnp.concatenate([wanted[k, i * half:(i + 1) * half, :] for k in ks], axis=1)
+            factor = 1.0 - asked * lax.rsqrt(real * real + imag * imag + 0.25)
             x = jnp.concatenate([real * factor, imag * factor], axis=0)
             sides.append(times_left(tables, i, x))
         add, sub = sides[0] + sides[1], sides[0] - sides[1]
-        real = jnp.concatenate([add[:half], sub[:half]], axis=0)
-        imag = jnp.concatenate([add[half:], sub[half:]], axis=0)
-        even = times_right(jnp.concatenate([real[:, :half], imag[:, :half]], axis=1), tables, 2)
-        odd = times_right(jnp.concatenate([real[:, half:], imag[:, half:]], axis=1), tables, 3)
-        alive = live(k, count_s[0, 0])
-        add, sub = (even + odd) * alive, (even - odd) * alive
-        real = jnp.concatenate([add[:, :half], sub[:, :half]], axis=1)
-        imag = jnp.concatenate([add[:, half:], sub[:, half:]], axis=1)
-        back[k, 0] = real
-        back[k, 1] = imag
-        w_r, w_i = window[k, 0], window[k, 1]
-        row, col = rows_s[0, 0, k], cols_s[0, 0, k]
-        shape = grad.shape[1:]
-        grad[0] += turned_back(w_r * real + w_i * imag, row, col).reshape(shape)
-        grad[1] += turned_back(w_r * imag - w_i * real, row, col).reshape(shape)
+        outs = []
+        for i in (0, 1):
+            rows = []
+            for j in range(together):
+                lanes = slice(j * frame + i * half, j * frame + (i + 1) * half)
+                rows += [jnp.concatenate([x[:half, lanes], x[half:, lanes]], axis=1) for x in (add, sub)]
+            outs.append(times_right(jnp.concatenate(rows, axis=0), tables, 2 + i))
+        for j, k in enumerate(ks):
+            rows = slice(j * frame, (j + 1) * frame)
+            even, odd = outs[0][rows], outs[1][rows]
+            alive = live(k, count_s[0, 0])
+            add, sub = (even + odd) * alive, (even - odd) * alive
+            real = jnp.concatenate([add[:, :half], sub[:, :half]], axis=1)
+            imag = jnp.concatenate([add[:, half:], sub[:, half:]], axis=1)
+            back[k, 0] = real
+            back[k, 1] = imag
+            w_r, w_i = window[k, 0], window[k, 1]
+            row, col = rows_s[0, 0, k], cols_s[0, 0, k]
+            shape = grad.shape[1:]
+            grad[0] += turned_back(w_r * real + w_i * imag, row, col).reshape(shape)
+            grad[1] += turned_back(w_r * imag - w_i * real, row, col).reshape(shape)
         return carry
 
-    lax.fori_loop(0, slots, one, 0, unroll=2)
+    lax.fori_loop(0, slots // together, few, 0)
 
     out_order = [flipped_by(z, SPREAD - 1 - t) for t in range(SPREAD)]
     for level in range(plan.levels):

time: 49.3 us -> 47.8 us (0.970)
  the two profiles are of different devices: /device:TPU:8 before, /device:TPU:1 now
where the time goes in v4:
time: 47.8 us; the launch traced here: 47.3 us
  Pallas kernels  44.2 us (92%)
  local copies, waits for them, and re-layouts  1.77 us (4%)
  between operations  1.29 us (3%)
    pallas_call x1, Pallas kernels, on_device(): pl.pallas_call(functools.partial(kernel, plan), out_shape=(jax.ShapeDtype...  44.2 us
    unnamed x2, local copies, waits for them, and re-layouts  1.77 us

profile of v4, /device:TPU:1, one launch (start us, length us, event | category | flops | bytes accessed | tf_op | source)
XLA Modules:
  0.0 47.3 jit_solution(1698347321810173781)
XLA Ops:
  1.3 44.2 %shard_map.86 = (f32[2,256,512]{2,1,0:T(8,128)S(1)}, f32[2,256,256]{2,1,0:T(8,128)S(1)}) custom-call(s32[1,1,4]{2,1,0:T(1,128)} %rows_h.1, s32[1,1,4]{2,1,0:T(1,128)} %cols_h.1, s32[1,1]{1,0:T(1,128)S(6)} %copy.11.count_h, f32[2,256,512]{2,1,0:T(8,128)} %field_h.1, f32[2,256,256]{2,1,0:T(8,128)} %probe_h.1, f32[4,256,256]{2,1,0:T(8,128)} %bitcast.1, ...), custom_call_target="tpu_custom_call" | custom-call | tf_op jit(solution)/shard_map/pallas_call | solution.py:584
  45.5 1.0 %copy.12 = f32[2,256,512]{2,1,0:T(8,128)} copy(f32[2,256,512]{2,1,0:T(8,128)S(1)} %get-tuple-element.4) | data formatting | bytes 2097152
  46.5 0.8 %copy.13 = f32[2,256,256]{2,1,0:T(8,128)} copy(f32[2,256,256]{2,1,0:T(8,128)S(1)} %get-tuple-element.5) | data formatting | bytes 1048576

commit v5 on v4

--- a/solution.py
+++ b/solution.py
@@ -19,7 +19,7 @@
 TOGETHER = 4
 EARLY = (0, 2)
 VMEM = 30 * 1024 * 1024
-PACE = (3, 1, 1, 3, 1, 1)
+PACE = (2, 1, 4, 4, 1, 0)
 
 
 def halves(x):
@@ -101,10 +101,10 @@
 
 def kernel(plan, rows_h, cols_h, count_h, field_h, probe_h, amps_h, tables_h, new_field, new_probe, *scratch):
     (
-        rows_s, cols_s, count_s, prior_rows, prior_cols, prior_count, field, rim, probe, amps, tables, rolled, window, wanted, spec, back,
+        twofold, rows_s, cols_s, count_s, prior_rows, prior_cols, prior_count, field, rim, probe, amps, tables, rolled, window, wanted, spec, back,
         left_side, weight, total, ahead, arrived, grad, halved, whole, final, gathered,
-    ) = scratch[:26]
-    rest = list(scratch[26:])
+    ) = scratch[:27]
+    rest = list(scratch[27:])
     came, held = rest.pop(0), rest.pop(0)
     twice = [rest.pop(0) for _ in plan.double]
     given = [rest.pop(0) for _ in plan.double]
@@ -220,10 +220,6 @@
 
     def turned(x, row, col):
         return pltpu.roll(pltpu.roll(x, row, 0), lax.rem(col, frame), 1)
-
-    def turned_back(x, row, col):
-        x = pltpu.roll(x, lax.rem(2 * frame - col, frame), 1)
-        return pltpu.roll(x, lax.rem(frame - row, frame), 0)
 
     for i in (0, 4, 5, 6):
         loads[i].wait()
@@ -325,7 +321,6 @@
 
     width = field.shape[2]
     lax.fori_loop(0, CHUNKS, first, 0)
-    grad[...] = jnp.zeros_like(grad)
 
     together = math.gcd(slots, TOGETHER)
 
@@ -360,11 +355,6 @@
             imag = jnp.concatenate([add[:, half:], sub[:, half:]], axis=1)
             back[k, 0] = real
             back[k, 1] = imag
-            w_r, w_i = window[k, 0], window[k, 1]
-            row, col = rows_s[0, 0, k], cols_s[0, 0, k]
-            shape = grad.shape[1:]
-            grad[0] += turned_back(w_r * real + w_i * imag, row, col).reshape(shape)
-            grad[1] += turned_back(w_r * imag - w_i * real, row, col).reshape(shape)
         return carry
 
     lax.fori_loop(0, slots // together, few, 0)
@@ -400,8 +390,25 @@
                 total_copy(c).start()
         sent[0] += count
 
+    def slope(plane):
+        sign = jnp.where(plane == 0, jnp.float32(1.0), jnp.float32(-1.0))
+        acc = None
+        for k in range(slots):
+            x = window[k, 0] * back[k, plane] + sign * (window[k, 1] * back[k, 1 - plane])
+            x = pltpu.roll(x, lax.rem(2 * frame - cols_s[0, 0, k], frame), 1)
+            for i in range(frame // 128):
+                lanes = x[:, i * 128:(i + 1) * 128]
+                twofold[k * 2 + i, :frame] = lanes
+                twofold[k * 2 + i, frame:] = lanes
+        for k in range(slots):
+            x = jnp.concatenate([twofold[k * 2 + i, pl.ds(rows_s[0, 0, k], frame), :] for i in range(frame // 128)], axis=1)
+            acc = x if acc is None else acc + x
+        grad[plane] = acc.reshape(grad.shape[1:])
+
+    slope(1 - core)
     for t in range(SPREAD):
         core_copy(t).start()
+    slope(core)
 
     def strip(s, carry):
         start = pl.multiple_of(s * STRIP, STRIP)
@@ -564,6 +571,7 @@
     operands = (row_offset, col_offset, frame_count, object_field, probe, amplitudes[0, 0], tables)
     doubles = max(1, len(plan.double))
     scratch = [
+        floats(slots * 2, 2 * frame, 128),
         *[pltpu.SMEM(x.shape, jnp.int32) for x in (row_offset, col_offset, frame_count)] * 2,
         floats(2, band, width), floats(2, band, width), floats(2, frame, frame), floats(slots, frame, frame),
         pltpu.VMEM(tables.shape, jnp.bfloat16),
@@ -581,7 +589,7 @@
         sems(2, SPREAD), sems(2, doubles), sems(2, SPREAD), sems(2, SPREAD, plan.others), sems(2, SPREAD),
         pltpu.SemaphoreType.REGULAR((plan.levels,)),
     ]
-    return pl.pallas_call(
+    results = pl.pallas_call(
         functools.partial(kernel, plan),
         out_shape=(
             jax.ShapeDtypeStruct(object_field.shape, jnp.float32),
@@ -594,6 +602,25 @@
             collective_id=0, has_side_effects=True, vmem_limit_bytes=VMEM
         ),
     )(*[x if x is frame_count else pltpu.with_memory_space_constraint(x, pltpu.HBM) for x in operands])
+    return pl.pallas_call(
+        deliver,
+        out_shape=tuple(jax.ShapeDtypeStruct(x.shape, x.dtype) for x in results),
+        in_specs=[vmem] * 2,
+        out_specs=(hbm,) * 2,
+        scratch_shapes=[sems(2, 2)],
+    )(*[pltpu.with_memory_space_constraint(x, pltpu.VMEM) for x in results])
+
+
+def deliver(*refs):
+    sources, targets, sem = refs[:2], refs[2:4], refs[4]
+    copies = [
+        pltpu.make_async_copy(sources[i].at[plane], targets[i].at[plane], sem.at[i, plane])
+        for i in (0, 1) for plane in (0, 1)
+    ]
+    for copy in copies:
+        copy.start()
+    for copy in copies:
+        copy.wait()
 
 
 def solution(mesh):

time: 47.8 us -> 47.1 us (0.985)
  local copies, waits for them, and re-layouts: 1.77 us -> 0 us
  Pallas kernels: 44.2 us -> 45.6 us
    unnamed x2 -> x0, local copies, waits for them, and re-layouts: 1.77 us -> none
    pallas_call x0 -> x1, Pallas kernels: none -> 1.17 us  [on_device(): pl.pallas_call(deliver, out_shape=tuple((jax.ShapeDtypeStruct(x.shape, x....]
where the time goes in v5:
time: 47.1 us; the launch traced here: 46.9 us
  Pallas kernels  45.6 us (97%)
  between operations  1.29 us (3%)
    pallas_call x1, Pallas kernels, on_device(): pl.pallas_call(functools.partial(kernel, plan), out_shape=(jax.ShapeDtype...  44.5 us
    pallas_call x1, Pallas kernels, on_device(): pl.pallas_call(deliver, out_shape=tuple((jax.ShapeDtypeStruct(x.shape, x....  1.17 us

profile of v5, /device:TPU:1, one launch (start us, length us, event | category | flops | bytes accessed | tf_op | source)
XLA Modules:
  0.0 46.9 jit_solution(1664533010834871710)
XLA Ops:
  1.3 44.5 %shard_map.86 = (f32[2,256,512]{2,1,0:T(8,128)S(1)}, f32[2,256,256]{2,1,0:T(8,128)S(1)}) custom-call(s32[1,1,4]{2,1,0:T(1,128)} %rows_h.1, s32[1,1,4]{2,1,0:T(1,128)} %cols_h.1, s32[1,1]{1,0:T(1,128)S(6)} %copy.9.count_h, f32[2,256,512]{2,1,0:T(8,128)} %field_h.1, f32[2,256,256]{2,1,0:T(8,128)} %probe_h.1, f32[4,256,256]{2,1,0:T(8,128)} %bitcast.1, ...), custom_call_target="tpu_custom_call" | custom-call | tf_op jit(solution)/shard_map/pallas_call | solution.py:592
  45.7 1.2 %shard_map.87 = (f32[2,256,512]{2,1,0:T(8,128)}, f32[2,256,256]{2,1,0:T(8,128)}) custom-call(f32[2,256,512]{2,1,0:T(8,128)S(1)} %get-tuple-element.4.refs_0_, f32[2,256,256]{2,1,0:T(8,128)S(1)} %get-tuple-element.5.refs_1_), custom_call_target="tpu_custom_call" | custom-call | tf_op jit(solution)/shard_map/pallas_call | solution.py:605

commit v6 on v5

--- a/solution.py
+++ b/solution.py
@@ -14,12 +14,12 @@
 TILE = 8
 CHUNKS = 4
 STRIP = 16
-TOTALS = 16
+TOTALS = 32
 UPDATES = 4
 TOGETHER = 4
 EARLY = (0, 2)
 VMEM = 30 * 1024 * 1024
-PACE = (2, 1, 4, 4, 1, 0)
+PACE = (4, 2, 6, 8, 2, 1)
 
 
 def halves(x):

time: 47.1 us -> 47.1 us (level)
  no operation moved by 1% of the time
where the time goes in v6:
time: 47.1 us; the launch traced here: 46.8 us
  Pallas kernels  45.5 us (97%)
  between operations  1.29 us (3%)
    pallas_call x1, Pallas kernels, on_device(): pl.pallas_call(functools.partial(kernel, plan), out_shape=(jax.ShapeDtype...  44.3 us
    pallas_call x1, Pallas kernels, on_device(): pl.pallas_call(deliver, out_shape=tuple((jax.ShapeDtypeStruct(x.shape, x....  1.17 us

profile of v6, /device:TPU:1, one launch (start us, length us, event | category | flops | bytes accessed | tf_op | source)
XLA Modules:
  0.0 46.8 jit_solution(14803314123951195883)
XLA Ops:
  1.3 44.3 %shard_map.86 = (f32[2,256,512]{2,1,0:T(8,128)S(1)}, f32[2,256,256]{2,1,0:T(8,128)S(1)}) custom-call(s32[1,1,4]{2,1,0:T(1,128)} %rows_h.1, s32[1,1,4]{2,1,0:T(1,128)} %cols_h.1, s32[1,1]{1,0:T(1,128)S(6)} %copy.9.count_h, f32[2,256,512]{2,1,0:T(8,128)} %field_h.1, f32[2,256,256]{2,1,0:T(8,128)} %probe_h.1, f32[4,256,256]{2,1,0:T(8,128)} %bitcast.1, ...), custom_call_target="tpu_custom_call" | custom-call | tf_op jit(solution)/shard_map/pallas_call | solution.py:592
  45.6 1.2 %shard_map.87 = (f32[2,256,512]{2,1,0:T(8,128)}, f32[2,256,256]{2,1,0:T(8,128)}) custom-call(f32[2,256,512]{2,1,0:T(8,128)S(1)} %get-tuple-element.4.refs_0_, f32[2,256,256]{2,1,0:T(8,128)S(1)} %get-tuple-element.5.refs_1_), custom_call_target="tpu_custom_call" | custom-call | tf_op jit(solution)/shard_map/pallas_call | solution.py:605
